TPU v7x, 512 devices: a 8x2x16 block of a 8x16x16 slice. The times are simulated.
512 devices in a mesh: parts: 2 (over y), rows: 16 (over x, core), cols: 16 (over z).
Axes of the slice: x: 8, y: 2, z: 16, core: 2. Of those that a mesh axis runs over, the one named last changes fastest.
The devices are a block of a 8x16x16 slice.
Arguments:
- singles: bfloat16 [4096, 384], P(('parts', 'rows', 'cols')), parts along dimension 0, may hold values from -120 to 120
- pair: bfloat16 [4096, 2048, 128], P(('parts', 'rows'), 'cols'), parts along dimension 0, may hold values from -6 to 6
- chain_sizes: int32 [16], P('parts'), parts along dimension 0, may hold values from 1 to 512, 2048 in all
- single_proj: bfloat16 [384, 1536], replicated, may hold values from -1 to 1
- query_bias: float32 [384], replicated, may hold values from -5 to 5
- pair_proj: bfloat16 [128, 16], replicated, may hold values from -0.5 to 0.5
- out_proj: bfloat16 [384, 384], replicated, may hold values from -1.25 to 1.25
Outputs:
- update: bfloat16 [4096, 384], P(('parts', 'rows', 'cols')), parts along dimension 0
There are 2 independent parts, one for each index of `parts`. A program takes and returns all parts, laid end to end along the dimension named above; an argument that names none is the same for every part. Nothing has to cross between parts.
Inputs may be any that keep to these rules, and one draw needn't show every extreme that they name: `chain_sizes`: the first 7 entries count the tokens of the chains in order; the last one counts the padding tokens at the end of the complex.
All inputs are finite; a program needn't handle non-finite values.
Results may differ from a plain program's by a relative error of at most 0.004.
The roundings to bfloat16 on the way count: a program that leaves them out, or rounds other values in their place, can miss the bound.
Values may be sent and summed in bfloat16 or wider, within the bound.
A program may use at most 64 MiB of HBM per device.

v0:
```python
import math

import jax
import jax.numpy as jnp
from jax import lax
from jax.sharding import PartitionSpec as P


def from_everyone(x, axis):
    copies = jnp.broadcast_to(x, (lax.axis_size(axis), *x.shape))
    return lax.all_to_all(copies, axis, split_axis=0, concat_axis=0, tiled=True)


def laid_out(blocks, dim):
    blocks = jnp.moveaxis(blocks, 0, dim)
    dims = blocks.shape
    return blocks.reshape(*dims[:dim], dims[dim] * dims[dim + 1], *dims[dim + 2 :])


def gather_directly(x, axis, dim):
    blocks = from_everyone(x, axis)
    return laid_out(blocks, dim)


def from_root(x, axis, root):
    return lax.dynamic_index_in_dim(lax.all_gather(x, axis), root, 0, keepdims=False)


def taken_together(x, axis):
    return from_everyone(x, axis).max(axis=0)


def split_up(x, dim, devices):
    dims = x.shape
    blocks = x.reshape(*dims[:dim], devices, dims[dim] // devices, *dims[dim + 1 :])
    return jnp.moveaxis(blocks, dim, 0)


def sum_at_owner(x, axis, dim):
    blocks = split_up(x, dim, lax.axis_size(axis))
    arrived = lax.all_to_all(blocks, axis, split_axis=0, concat_axis=0, tiled=True)
    return arrived.sum(axis=0)


def side_by_side(arrays, axis, dim, along):
    both = jnp.concatenate(arrays, axis=along)
    out, at, outs = (sum_at_owner(both, axis, dim), 0, [])
    for a in arrays:
        outs.append(lax.slice_in_dim(out, at, at + a.shape[along], axis=along))
        at += a.shape[along]
    return tuple(outs)


def normalize(matrix):
    average = jnp.mean(matrix, axis=-1, keepdims=True)
    centered = matrix - average
    variance = jnp.mean(centered * centered, axis=-1, keepdims=True)
    return centered * lax.rsqrt(variance + 1e-05)


def tile_bias(pair, pair_proj):
    tile_rows, tile_cols, channels = pair.shape
    head_count = pair_proj.shape[1]
    row_block = math.gcd(tile_rows, 32)
    blocks = pair.reshape(tile_rows // row_block, row_block, tile_cols, channels)

    def project(pair_rows):
        pair_normed = normalize(pair_rows.astype(jnp.float32)).astype(jnp.bfloat16)
        return jnp.einsum(
            "ikc,ch->hik", pair_normed, pair_proj, preferred_element_type=jnp.float32
        ).astype(jnp.bfloat16)

    stacked = lax.map(project, blocks)
    return jnp.moveaxis(stacked, 1, 0).reshape(head_count, tile_rows, tile_cols)


def tile_scores(query_slab, key_side, bias_tile, live_count, column, head_count, score_scale):
    tile_rows, features = query_slab.shape
    tile_cols = key_side.shape[0]
    head_dim = features // head_count
    query_heads = query_slab.reshape(tile_rows, head_count, head_dim)
    key_heads = key_side[:, :features].reshape(tile_cols, head_count, head_dim)
    scores = jnp.einsum(
        "qhd,khd->hqk", query_heads, key_heads, preferred_element_type=jnp.float32
    ) * score_scale + bias_tile.astype(jnp.float32)
    key_live = column * tile_cols + jnp.arange(tile_cols, dtype=jnp.int32) < live_count
    return jnp.where(key_live[None, None, :], scores, -1e30)


def tile_terms(scores, maxima, key_side, head_count):
    tile_cols, doubled = key_side.shape
    features = doubled // 2
    head_dim = features // head_count
    value_heads = key_side[:, features:].reshape(tile_cols, head_count, head_dim)
    weights = jnp.exp(scores - maxima[:, :, None])
    totals = jnp.transpose(jnp.sum(weights, axis=-1))
    numerator = jnp.einsum(
        "hqk,khd->qhd",
        weights.astype(jnp.bfloat16),
        value_heads,
        preferred_element_type=jnp.float32,
    )
    return (numerator.reshape(scores.shape[1], features), totals)


def shards(singles, pair, chain_sizes, single_proj, query_bias, pair_proj, out_proj):
    own_rows, features = singles.shape
    head_count = pair_proj.shape[1]
    head_dim = features // head_count
    score_scale = head_dim ** (-0.5)
    normed = normalize(singles.astype(jnp.float32)).astype(jnp.bfloat16)
    projected = jnp.dot(normed, single_proj, preferred_element_type=jnp.float32)
    gating = jax.nn.sigmoid(projected[:, 3 * features :])
    live_count = jnp.sum(chain_sizes[:-1])
    bias_tile = tile_bias(pair, pair_proj)
    slab_rows = gather_directly(normed, "cols", 0)
    column = lax.axis_index("cols")
    key_normed_rows = from_root(slab_rows, "rows", column)
    query_slab = (
        jnp.dot(slab_rows, single_proj[:, :features], preferred_element_type=jnp.float32)
        + query_bias
    ).astype(jnp.bfloat16)
    key_side = jnp.dot(
        key_normed_rows, single_proj[:, features : 3 * features], preferred_element_type=jnp.float32
    ).astype(jnp.bfloat16)
    scores = tile_scores(
        query_slab, key_side, bias_tile, live_count, column, head_count, score_scale
    )
    maxima = taken_together(jnp.max(scores, axis=-1), "cols")
    numerator, totals = tile_terms(scores, maxima, key_side, head_count)
    numerator_own, totals_own = side_by_side((numerator, totals), "cols", 0, 1)
    averaged = (
        numerator_own.reshape(own_rows, head_count, head_dim) / totals_own[:, :, None]
    ).reshape(own_rows, features)
    attended = (gating * averaged).astype(jnp.bfloat16)
    return jnp.dot(attended, out_proj, preferred_element_type=jnp.float32).astype(jnp.bfloat16)


def solution(mesh):
    placed = (
        P(("parts", "rows", "cols"), None),
        P(("parts", "rows"), "cols", None),
        P("parts"),
        P(),
        P(),
        P(),
        P(),
    )
    return jax.shard_map(
        shards,
        mesh=mesh,
        in_specs=placed,
        out_specs=P(("parts", "rows", "cols"), None),
        check_vma=False,
    )
```

profile of v0, /device:TPU:66, one launch (start us, length us, event | category | flops | bytes accessed | tf_op | source)
XLA Modules:
  0.0 169.4 jit_solution(11094891388623381170)
XLA Ops:
  6.6 0.9 convert_reduce_fusion.1
  7.4 0.9 fusion.33
  8.3 0.8 fusion.34
  9.1 0.6 broadcast_in_dim.33
  9.7 43.7 %all-to-all-start = ((bf16[16,8,384]{2,1,0:T(8,128)(2,1)}), bf16[16,8,384]{2,1,0:T(8,128)(2,1)S(1)}, u32[]{:S(2)}, u32[]{:S(2)}) async-start(bf16[16,8,384]{2,1,0:T(8,128)(2,1)} %broadcast_in_dim.33), calls=%async_computation | async-start | bytes 196608 | tf_op jit(solution)/shard_map/all_to_all | solution.py:11
  53.5 13.4 %all-to-all-done = bf16[16,8,384]{2,1,0:T(8,128)(2,1)S(1)} async-done(((bf16[16,8,384]{2,1,0:T(8,128)(2,1)}), bf16[16,8,384]{2,1,0:T(8,128)(2,1)S(1)}, u32[]{:S(2)}, u32[]{:S(2)}) %all-to-all-start) | async-done | bytes 98336 | tf_op jit(solution)/shard_map/all_to_all | solution.py:11
  66.9 0.6 copy-done.1
  67.6 26.2 %while.10 = (s32[]{:T(128)}, bf16[4,16,32,128]{3,2,0,1:T(8,128)(2,1)S(1)}, bf16[4,32,128,128]{3,2,1,0:T(8,128)(2,1)}, bf16[128,16]{0,1:T(8,128)(2,1)}, s32[]{:T(128)}) while((s32[]{:T(128)}, bf16[4,16,32,128]{3,2,0,1:T(8,128)(2,1)S(1)}, bf16[4,32,128,128]{3,2,1,0:T(8,128)(2,1)}, bf16[128,16]{0,1:T(8,128)(2,1)}, s32[]{:T(128)}) %tuple.25), condition=%wide.region_6.7_spmd, body=%wide.region_3.6_spmd.sunk | while | flops 22089728 | bytes 3706993 | solution.py:73
  67.6 1.6 convert_reduce_fusion.3
  69.2 2.3 %fusion.51 = f32[32,128]{1,0:T(8,128)S(1)} fusion(f32[32,128]{1,0:T(8,128)S(1)} %broadcast_multiply_fusion.3, bf16[4,32,128,128]{3,2,1,0:T(8,128)(2,1)} %get-tuple-element.77, s32[]{:T(128)S(6)} %copy.45), kind=kLoop, calls=%fused_computation.5.clone.1 | loop fusion | flops 2093056 | bytes 1081348 | tf_op jit(solution)/shard_map/while/body/eval_jaxpr/reduce_sum | solution.py:57
  71.6 2.5 %fusion.52 = bf16[1,16,32,128]{3,1,2,0:T(8,128)(2,1)S(1)} fusion(f32[32,128]{1,0:T(8,128)S(1)} %add_rsqrt_fusion.3, f32[32,128]{1,0:T(8,128)S(1)} %broadcast_multiply_fusion.3, bf16[4,32,128,128]{3,2,1,0:T(8,128)(2,1)} %get-tuple-element.77, s32[]{:T(128)S(6)} %copy.45, bf16[128,16]{0,1:T(8,128)(2,1)S(1)} %copy-done.3), kind=kOutput, calls=%fused_computation.8.clone.1 | convolution fusion | flops 18939904 | bytes 1216516 | tf_op jit(solution)/shard_map/while/body/eval_jaxpr/ikc,ch->hik/dot_general | solution.py:69
  74.2 1.6 convert_reduce_fusion.3
  75.8 2.3 %fusion.51 = f32[32,128]{1,0:T(8,128)S(1)} fusion(f32[32,128]{1,0:T(8,128)S(1)} %broadcast_multiply_fusion.3, bf16[4,32,128,128]{3,2,1,0:T(8,128)(2,1)} %get-tuple-element.77, s32[]{:T(128)S(6)} %copy.45), kind=kLoop, calls=%fused_computation.5.clone.1 | loop fusion | flops 2093056 | bytes 1081348 | tf_op jit(solution)/shard_map/while/body/eval_jaxpr/reduce_sum | solution.py:57
  78.1 2.5 %fusion.52 = bf16[1,16,32,128]{3,1,2,0:T(8,128)(2,1)S(1)} fusion(f32[32,128]{1,0:T(8,128)S(1)} %add_rsqrt_fusion.3, f32[32,128]{1,0:T(8,128)S(1)} %broadcast_multiply_fusion.3, bf16[4,32,128,128]{3,2,1,0:T(8,128)(2,1)} %get-tuple-element.77, s32[]{:T(128)S(6)} %copy.45, bf16[128,16]{0,1:T(8,128)(2,1)S(1)} %copy-done.3), kind=kOutput, calls=%fused_computation.8.clone.1 | convolution fusion | flops 18939904 | bytes 1216516 | tf_op jit(solution)/shard_map/while/body/eval_jaxpr/ikc,ch->hik/dot_general | solution.py:69
  80.7 1.6 convert_reduce_fusion.3
  82.3 2.3 %fusion.51 = f32[32,128]{1,0:T(8,128)S(1)} fusion(f32[32,128]{1,0:T(8,128)S(1)} %broadcast_multiply_fusion.3, bf16[4,32,128,128]{3,2,1,0:T(8,128)(2,1)} %get-tuple-element.77, s32[]{:T(128)S(6)} %copy.45), kind=kLoop, calls=%fused_computation.5.clone.1 | loop fusion | flops 2093056 | bytes 1081348 | tf_op jit(solution)/shard_map/while/body/eval_jaxpr/reduce_sum | solution.py:57
  84.7 2.5 %fusion.52 = bf16[1,16,32,128]{3,1,2,0:T(8,128)(2,1)S(1)} fusion(f32[32,128]{1,0:T(8,128)S(1)} %add_rsqrt_fusion.3, f32[32,128]{1,0:T(8,128)S(1)} %broadcast_multiply_fusion.3, bf16[4,32,128,128]{3,2,1,0:T(8,128)(2,1)} %get-tuple-element.77, s32[]{:T(128)S(6)} %copy.45, bf16[128,16]{0,1:T(8,128)(2,1)S(1)} %copy-done.3), kind=kOutput, calls=%fused_computation.8.clone.1 | convolution fusion | flops 18939904 | bytes 1216516 | tf_op jit(solution)/shard_map/while/body/eval_jaxpr/ikc,ch->hik/dot_general | solution.py:69
  87.2 1.6 convert_reduce_fusion.3
  88.8 2.3 %fusion.51 = f32[32,128]{1,0:T(8,128)S(1)} fusion(f32[32,128]{1,0:T(8,128)S(1)} %broadcast_multiply_fusion.3, bf16[4,32,128,128]{3,2,1,0:T(8,128)(2,1)} %get-tuple-element.77, s32[]{:T(128)S(6)} %copy.45), kind=kLoop, calls=%fused_computation.5.clone.1 | loop fusion | flops 2093056 | bytes 1081348 | tf_op jit(solution)/shard_map/while/body/eval_jaxpr/reduce_sum | solution.py:57
  91.2 2.5 %fusion.52 = bf16[1,16,32,128]{3,1,2,0:T(8,128)(2,1)S(1)} fusion(f32[32,128]{1,0:T(8,128)S(1)} %add_rsqrt_fusion.3, f32[32,128]{1,0:T(8,128)S(1)} %broadcast_multiply_fusion.3, bf16[4,32,128,128]{3,2,1,0:T(8,128)(2,1)} %get-tuple-element.77, s32[]{:T(128)S(6)} %copy.45, bf16[128,16]{0,1:T(8,128)(2,1)S(1)} %copy-done.3), kind=kOutput, calls=%fused_computation.8.clone.1 | convolution fusion | flops 18939904 | bytes 1216516 | tf_op jit(solution)/shard_map/while/body/eval_jaxpr/ikc,ch->hik/dot_general | solution.py:69
  94.4 0.6 slice_reduce_fusion
  95.1 0.7 add_compare_fusion
  95.7 1.2 fusion.14
  97.0 9.3 %all-gather.2.cloned.1.call-done = bf16[16,128,384]{2,1,0:T(8,128)(2,1)} async-done(((bf16[1,128,384]{2,1,0:T(8,128)(2,1)}), bf16[16,128,384]{2,1,0:T(8,128)(2,1)}) %all-gather.2.cloned.1.call-update) | async-done | bytes 1572880 | tf_op jit(solution)/shard_map/all_gather | solution.py:26
  106.3 1.4 convolution_convert_fusion.1
  108.3 0.7 broadcast_in_dim.37
  109.0 13.0 %all-to-all-start.1 = ((f32[16,16,128]{2,1,0:T(8,128)}), f32[16,16,128]{2,1,0:T(8,128)S(1)}, u32[]{:S(2)}, u32[]{:S(2)}) async-start(f32[16,16,128]{2,1,0:T(8,128)} %broadcast_in_dim.37), calls=%async_computation.1 | async-start | bytes 262144 | tf_op jit(solution)/shard_map/all_to_all | solution.py:11
  122.1 14.5 %all-to-all-done.1 = f32[16,16,128]{2,1,0:T(8,128)S(1)} async-done(((f32[16,16,128]{2,1,0:T(8,128)}), f32[16,16,128]{2,1,0:T(8,128)S(1)}, u32[]{:S(2)}, u32[]{:S(2)}) %all-to-all-start.1) | async-done | bytes 131104 | tf_op jit(solution)/shard_map/all_to_all | solution.py:11
  137.1 0.5 copy.34
  137.6 0.5 concatenate.8
  138.2 22.3 %all_to_all.15 = f32[16,8,400]{2,1,0:T(8,128)S(1)} all-to-all(f32[16,8,400]{2,1,0:T(8,128)S(1)} %pad_maximum_fusion), channel_id=1, replica_groups=mesh['parts'=2,'rows'=16,'cols'=16] {'cols'}, dimensions={0} | all-to-all | bytes 409600 | tf_op jit(solution)/shard_map/all_to_all | solution.py:41
  160.7 1.9 %convolution_convert_fusion.2 = bf16[8,384]{1,0:T(8,128)(2,1)} fusion(bf16[384,384]{1,0:T(8,128)(2,1)S(1)} %copy-done, bf16[8,384]{1,0:T(8,128)(2,1)S(1)} %fusion.34, bf16[384,1536]{1,0:T(8,128)(2,1)} %param.12, f32[8,384]{1,0:T(8,128)S(1)} %div.30, f32[8,400]{1,0:T(8,128)S(1)} %reduce_sum.67), kind=kOutput, calls=%fused_computation.30 | convolution fusion | flops 4740096 | bytes 626688 | tf_op jit(solution)/shard_map/dot_general | solution.py:136
  (50 shorter events, 2.6 us)
Async XLA Ops:
  6.5 154.1 %copy-start = (bf16[384,384]{1,0:T(8,128)(2,1)S(1)}, bf16[384,384]{1,0:T(8,128)(2,1)}, u32[]{:S(2)}) copy-start(bf16[384,384]{1,0:T(8,128)(2,1)} %param.15) | copy-start | bytes 884740
  9.7 57.2 %all-to-all-start = ((bf16[16,8,384]{2,1,0:T(8,128)(2,1)}), bf16[16,8,384]{2,1,0:T(8,128)(2,1)S(1)}, u32[]{:S(2)}, u32[]{:S(2)}) async-start(bf16[16,8,384]{2,1,0:T(8,128)(2,1)} %broadcast_in_dim.33), calls=%async_computation | async-start | bytes 196608 | tf_op jit(solution)/shard_map/all_to_all | solution.py:11
  53.4 53.0 %all-gather.2.cloned.1.call-start = ((), (), s32[]{:S(2)}) async-start(), calls=%async_computation.3 | async-start | bytes 1671168 | tf_op jit(solution)/shard_map/all_gather | solution.py:26
  66.9 0.6 copy-start.1
  67.6 4.0 %copy-start.3 = (bf16[128,16]{0,1:T(8,128)(2,1)S(1)}, bf16[128,16]{0,1:T(8,128)(2,1)}, u32[]{:S(2)}) copy-start(bf16[128,16]{0,1:T(8,128)(2,1)} %get-tuple-element.78) | copy-start | bytes 12292 | tf_op jit(solution)/shard_map/while
  74.1 4.0 %copy-start.3 = (bf16[128,16]{0,1:T(8,128)(2,1)S(1)}, bf16[128,16]{0,1:T(8,128)(2,1)}, u32[]{:S(2)}) copy-start(bf16[128,16]{0,1:T(8,128)(2,1)} %get-tuple-element.78) | copy-start | bytes 12292 | tf_op jit(solution)/shard_map/while
  80.7 4.0 %copy-start.3 = (bf16[128,16]{0,1:T(8,128)(2,1)S(1)}, bf16[128,16]{0,1:T(8,128)(2,1)}, u32[]{:S(2)}) copy-start(bf16[128,16]{0,1:T(8,128)(2,1)} %get-tuple-element.78) | copy-start | bytes 12292 | tf_op jit(solution)/shard_map/while
  87.2 4.0 %copy-start.3 = (bf16[128,16]{0,1:T(8,128)(2,1)S(1)}, bf16[128,16]{0,1:T(8,128)(2,1)}, u32[]{:S(2)}) copy-start(bf16[128,16]{0,1:T(8,128)(2,1)} %get-tuple-element.78) | copy-start | bytes 12292 | tf_op jit(solution)/shard_map/while
  93.8 0.7 copy-start.5
  93.8 1.9 %copy-start.2 = (bf16[16,8,384]{2,1,0:T(8,128)(2,1)S(1)}, bf16[16,8,384]{2,1,0:T(8,128)(2,1)}, u32[]{:S(2)}) copy-start(bf16[16,8,384]{2,1,0:T(8,128)(2,1)} %copy-done.1) | copy-start | bytes 294916
  93.8 1.9 %copy-start.4 = (f32[384]{0:T(512)S(1)}, f32[384]{0:T(512)}, u32[]{:S(2)}) copy-start(f32[384]{0:T(512)} %param.13) | copy-start | bytes 4612
  109.0 27.6 %all-to-all-start.1 = ((f32[16,16,128]{2,1,0:T(8,128)}), f32[16,16,128]{2,1,0:T(8,128)S(1)}, u32[]{:S(2)}, u32[]{:S(2)}) async-start(f32[16,16,128]{2,1,0:T(8,128)} %broadcast_in_dim.37), calls=%async_computation.1 | async-start | bytes 262144 | tf_op jit(solution)/shard_map/all_to_all | solution.py:11
Sparse Core Ops, SparseCore 0:
  67.7 38.5 all-gather.1
where the time goes:
time: 170 us; the launch traced here: 169 us
  starting transfers between devices  56.8 us (33%)
  waiting for transfers between devices  37.3 us (22%)
  blocking collectives  22.3 us (13%)
  other arithmetic  19.8 us (12%)
  matrix products  15.1 us (9%)
  between operations  13.6 us (8%)
  local copies, waits for them, and re-layouts  4.31 us (3%)
    all_to_all x2, starting transfers between devices, from_everyone(): return lax.all_to_all(copies, axis, split_axis=0, concat_axis=0, tiled=True)  56.7 us
    all_to_all x2, waiting for transfers between devices, from_everyone(): return lax.all_to_all(copies, axis, split_axis=0, concat_axis=0, tiled=True)  27.9 us
    all_to_all x1, blocking collectives, sum_at_owner(): lax.all_to_all(blocks, axis, split_axis=0, concat_axis=0, tiled=True)  22.3 us
    reduce_sum x5, other arithmetic, normalize(): variance = jnp.mean(centered * centered, axis=-1, keepdims=True)  10.2 us
    dot_general x4, matrix products, project(): jnp.einsum('ikc,ch->hik', pair_normed, pair_proj, preferred_element_type=...  9.98 us
    all_gather x1, waiting for transfers between devices, from_root(): lax.all_gather(x, axis)  9.31 us
    reduce_sum x5, other arithmetic, normalize(): average = jnp.mean(matrix, axis=-1, keepdims=True)  7.16 us
  transfers between devices with their start and end apart: 3, of which 3 were waited for; matrix products, arithmetic and copies ran while one was open for 17% of the time, Pallas kernels for 0%

commit v1 on v0

v1 whole, which is shorter than its diff:
```python
import functools

import jax
import jax.numpy as jnp
from jax import lax
from jax.experimental import pallas as pl
from jax.experimental.pallas import tpu as pltpu
from jax.sharding import PartitionSpec as P

LANES = 128
MASKED = -1e30
FLOOR = -1e28
F32 = jnp.float32
BF16 = jnp.bfloat16


def peer(axis, index):
    return dict(device_id={axis: index}, device_id_type=pl.DeviceIdType.MESH)


def normalize(rows, axis):
    centered = rows - jnp.mean(rows, axis=axis, keepdims=True)
    variance = jnp.mean(centered * centered, axis=axis, keepdims=True)
    return centered * lax.rsqrt(variance + 1e-05)


def matmul(a, b):
    return jnp.dot(a, b, preferred_element_type=F32)


def iota(shape, dim):
    return lax.broadcasted_iota(jnp.int32, shape, dim)


def flat(blocks):
    count, rows, width = blocks.shape
    return blocks.astype(F32).reshape(count * rows, width).astype(BF16)


def kernel(
    rows_n,
    cols_n,
    chunks,
    singles,
    pair,
    chain,
    proj,
    q_bias,
    pair_proj,
    out_proj,
    out,
    own_v,
    pair_v,
    chain_s,
    proj_v,
    q_bias_v,
    pair_proj_v,
    out_proj_v,
    query_in,
    row_in,
    key_in,
    bias_v,
    score_v,
    weight_v,
    value_v,
    part_out,
    part_in,
    load_sem,
    pair_sem,
    query_send,
    query_recv,
    row_send,
    row_recv,
    key_send,
    key_recv,
    part_send,
    part_recv,
):
    own, features = own_v.shape
    tile_rows, tile_cols, channels = pair_v.shape
    heads = pair_proj_v.shape[1]
    head_dim = features // heads
    lane_blocks = features // LANES
    slots = chain_s.shape[0]
    scale = head_dim ** (-0.5)
    row = lax.axis_index("rows")
    col = lax.axis_index("cols")

    loads = [
        pltpu.make_async_copy(src, dst, load_sem.at[n])
        for n, (src, dst) in enumerate(
            [
                (singles, own_v),
                (pair_proj, pair_proj_v),
                (proj, proj_v),
                (q_bias, q_bias_v),
                (out_proj, out_proj_v),
                (chain, chain_s),
            ]
        )
    ]
    step = tile_rows // chunks
    pieces = [
        pltpu.make_async_copy(
            pair.at[pl.ds(n * step, step)], pair_v.at[pl.ds(n * step, step)], pair_sem.at[n]
        )
        for n in range(chunks)
    ]
    loads[0].start()
    loads[1].start()
    pieces[0].start()
    for load in loads[2:]:
        load.start()
    for piece in pieces[1:]:
        piece.start()

    barrier = pltpu.get_barrier_semaphore()
    for d in range(1, cols_n):
        pl.semaphore_signal(barrier, inc=1, **peer("cols", lax.rem(col + d, cols_n)))
    for d in range(1, rows_n):
        pl.semaphore_signal(barrier, inc=1, **peer("rows", lax.rem(row + d, rows_n)))

    def far_first(count):
        return sorted(range(1, count), key=lambda d: -min(d, count - d))

    def send(src, dst, sems, axis, index, mine, target):
        return pltpu.make_async_remote_copy(
            src_ref=src,
            dst_ref=dst,
            send_sem=sems[0].at[target],
            recv_sem=sems[1].at[mine],
            **peer(axis, index),
        )

    def query_copy(other):
        return send(
            query_in.at[col], query_in.at[col], (query_send, query_recv), "cols", other, col, other
        )

    def row_copy(other):
        return send(row_in.at[row], row_in.at[row], (row_send, row_recv), "rows", other, row, other)

    def key_copy(other):
        return send(row_in.at[other], key_in.at[col], (key_send, key_recv), "cols", other, col, other)

    def part_copy(other):
        return send(
            part_out.at[other], part_in.at[col], (part_send, part_recv), "cols", other, col, other
        )

    def arrival(buf, sems, axis, index):
        return send(buf.at[index], buf.at[index], sems, axis, index, index, index)

    loads[0].wait()
    normed = normalize(own_v[...].astype(F32), -1).astype(BF16)
    query_in[pl.ds(col, 1)] = normed[None]
    row_in[pl.ds(row, 1)] = normed[None]

    loads[1].wait()
    pair_w = jnp.transpose(pair_proj_v[...].astype(F32)).astype(BF16)

    def tile_bias(first, last):
        @pl.loop(first, last, unroll=2)
        def _(i):
            block = jnp.transpose(pair_v[i]).astype(F32)
            block_normed = normalize(block, 0).astype(BF16)
            bias = matmul(pair_w, block_normed)
            bias_v[pl.ds(pl.multiple_of(i * heads, heads), heads), :] = bias.astype(BF16).astype(F32)

    def bias_chunks(first, last):
        for n in range(first, last):
            pieces[n].wait()
            tile_bias(n * step, (n + 1) * step)

    bias_chunks(0, chunks // 4)
    pl.semaphore_wait(barrier, cols_n + rows_n - 2)
    for d in far_first(rows_n):
        row_copy(lax.rem(row + d, rows_n)).start()
    for d in far_first(cols_n):
        query_copy(lax.rem(col + d, cols_n)).start()

    loads[2].wait()
    loads[3].wait()
    own_gate = jax.nn.sigmoid(matmul(normed, proj_v[:, 3 * features :]))
    bias_chunks(chunks // 4, chunks // 2)

    for d in range(1, rows_n):
        arrival(row_in, (row_send, row_recv), "rows", lax.rem(row + d, rows_n)).wait_recv()
    for d in far_first(cols_n):
        key_copy(lax.rem(col + d, cols_n)).start()
    key_in[pl.ds(col, 1)] = row_in[pl.ds(col, 1)]
    bias_chunks(chunks // 2, chunks)

    for d in range(1, cols_n):
        arrival(query_in, (query_send, query_recv), "cols", lax.rem(col + d, cols_n)).wait_recv()
    queries = (
        matmul(flat(query_in[...]), proj_v[:, :features]) + q_bias_v[...]
    ).astype(BF16).astype(F32)
    for d in range(1, cols_n):
        arrival(key_in, (key_send, key_recv), "cols", lax.rem(col + d, cols_n)).wait_recv()
    key_side = matmul(flat(key_in[...]), proj_v[:, features : 3 * features]).astype(BF16)
    keys = key_side[:, :features]
    values = key_side[:, features:].astype(F32)

    def heads_of(b):
        return [
            h
            for h in range(heads)
            if h * head_dim < (b + 1) * LANES and (h + 1) * head_dim > b * LANES
        ]

    def head_lanes(b, h):
        feature = iota((1, LANES), 1) + b * LANES
        return (feature >= h * head_dim) & (feature < (h + 1) * head_dim)

    seen = set()
    for b in range(lane_blocks):
        members = heads_of(b)
        block = slice(b * LANES, (b + 1) * LANES)
        stacked = jnp.concatenate(
            [jnp.where(head_lanes(b, h), queries[:, block], 0.0).astype(BF16) for h in members], axis=0
        )
        scores = lax.dot_general(
            stacked, keys[:, block], (((1,), (1,)), ((), ())), preferred_element_type=F32
        )
        for n, h in enumerate(members):
            part = scores[n * tile_rows : (n + 1) * tile_rows]
            score_v[h] = score_v[h] + part if h in seen else part
            seen.add(h)
            value_v[b, n * tile_cols : (n + 1) * tile_cols, :] = jnp.where(
                head_lanes(b, h), values[:, block], 0.0
            ).astype(BF16)

    loads[5].wait()
    live = chain_s[0]
    for n in range(1, slots - 1):
        live = live + chain_s[n]
    key_live = iota((1, tile_cols), 1) + col * tile_cols < live
    lane = iota((1, LANES), 1)
    top = jnp.zeros((tile_rows, LANES), F32)
    for h in range(heads):
        scores = score_v[h] * scale + bias_v[pl.ds(h, tile_rows, stride=heads), :]
        scores = jnp.where(key_live, scores, MASKED)
        largest = jnp.maximum(jnp.max(scores, axis=-1, keepdims=True), FLOOR)
        weight_v[:, h * tile_cols : (h + 1) * tile_cols] = jnp.exp(scores - largest).astype(BF16)
        top = jnp.where(lax.rem(lane, heads) == h, largest, top)

    ones_row = lax.div(iota((heads * tile_cols, LANES), 0), tile_cols)
    ones_lane = iota((heads * tile_cols, LANES), 1)
    ones = jnp.where(
        (lax.rem(ones_lane, heads) == ones_row) & (ones_lane < 2 * heads), 1.0, 0.0
    ).astype(BF16)
    stats = jnp.where(lane < 2 * heads, matmul(weight_v[...], ones), top)
    first = stats.astype(BF16).astype(F32)
    second = (stats - first).astype(BF16).astype(F32)
    third = stats - first - second
    group = lax.div(lane, heads)
    stats = jnp.where(
        (group == 0) | (group == 2), first, jnp.where((group == 1) | (group == 3), second, third)
    )
    stats = jnp.where(group < 5, stats, 0.0).astype(BF16)
    own_rows = tile_rows // cols_n
    part_out[:, :, features:] = stats.astype(F32).reshape(cols_n, own_rows, LANES).astype(BF16)
    for b in range(lane_blocks):
        members = heads_of(b)
        summed = matmul(
            weight_v[:, members[0] * tile_cols : (members[-1] + 1) * tile_cols],
            value_v[b, : len(members) * tile_cols, :],
        )
        part_out[:, :, b * LANES : (b + 1) * LANES] = summed.reshape(
            cols_n, own_rows, LANES
        ).astype(BF16)

    part_in[pl.ds(col, 1)] = part_out[pl.ds(col, 1)]
    for d in far_first(cols_n):
        part_copy(lax.rem(col + d, cols_n)).start()
    loads[4].wait()
    spread_row = iota((LANES, features), 0)
    spread_head = lax.div(iota((LANES, features), 1), head_dim)
    matches = lax.rem(spread_row, heads) == spread_head
    spread_group = lax.div(spread_row, heads)
    to_total = jnp.where(matches & (spread_group < 2), 1.0, 0.0).astype(BF16)
    to_top = jnp.where(matches & (spread_group >= 2) & (spread_group < 5), 1.0, 0.0).astype(BF16)
    for d in range(1, cols_n):
        arrival(part_in, (part_send, part_recv), "cols", lax.rem(col + d, cols_n)).wait_recv()
    arrived = flat(part_in[:, :, features:])
    total = matmul(arrived, to_total).reshape(cols_n, own_rows, features)
    tops = matmul(arrived, to_top).reshape(cols_n, own_rows, features)
    factor = jnp.exp(tops - jnp.max(tops, axis=0, keepdims=True))
    total = jnp.sum(factor * total, axis=0)
    numerator = jnp.sum(factor * part_in[:, :, :features].astype(F32), axis=0)
    attended = (own_gate * (numerator / total)).astype(BF16)
    out[...] = matmul(attended, out_proj_v[...]).astype(BF16)

    for d in range(1, rows_n):
        row_copy(lax.rem(row + d, rows_n)).wait_send()
    for d in range(1, cols_n):
        other = lax.rem(col + d, cols_n)
        query_copy(other).wait_send()
        key_copy(other).wait_send()
        part_copy(other).wait_send()


def shards(rows_n, cols_n, singles, pair, chain_sizes, single_proj, query_bias, pair_proj, out_proj):
    own, features = singles.shape
    tile_rows, tile_cols, channels = pair.shape
    heads = pair_proj.shape[1]
    chunks = 16
    dma = pltpu.SemaphoreType.DMA
    lane_blocks = features // LANES
    widest = -(-LANES // (features // heads)) + 1
    return pl.pallas_call(
        functools.partial(kernel, rows_n, cols_n, chunks),
        out_shape=jax.ShapeDtypeStruct((own, features), BF16),
        in_specs=[pl.BlockSpec(memory_space=pl.ANY)] * 7,
        out_specs=pl.BlockSpec(memory_space=pltpu.VMEM),
        scratch_shapes=[
            pltpu.VMEM((own, features), BF16),
            pltpu.VMEM(pair.shape, BF16),
            pltpu.SMEM(chain_sizes.shape, jnp.int32),
            pltpu.VMEM(single_proj.shape, BF16),
            pltpu.VMEM((1, features), F32),
            pltpu.VMEM(pair_proj.shape, BF16),
            pltpu.VMEM(out_proj.shape, BF16),
            pltpu.VMEM((cols_n, own, features), BF16),
            pltpu.VMEM((rows_n, own, features), BF16),
            pltpu.VMEM((cols_n, own, features), BF16),
            pltpu.VMEM((tile_rows * heads, tile_cols), F32),
            pltpu.VMEM((heads, tile_rows, tile_cols), F32),
            pltpu.VMEM((tile_rows, heads * tile_cols), BF16),
            pltpu.VMEM((lane_blocks, widest * tile_cols, LANES), BF16),
            pltpu.VMEM((cols_n, own, features + LANES), BF16),
            pltpu.VMEM((cols_n, own, features + LANES), BF16),
            dma((6,)),
            dma((chunks,)),
            dma((cols_n,)),
            dma((cols_n,)),
            dma((rows_n,)),
            dma((rows_n,)),
            dma((cols_n,)),
            dma((cols_n,)),
            dma((cols_n,)),
            dma((cols_n,)),
        ],
        compiler_params=pltpu.CompilerParams(collective_id=0, has_side_effects=True),
    )(singles, pair, chain_sizes, single_proj, query_bias.reshape(1, features), pair_proj, out_proj)


def solution(mesh):
    placed = (
        P(("parts", "rows", "cols"), None),
        P(("parts", "rows"), "cols", None),
        P("parts"),
        P(),
        P(),
        P(),
        P(),
    )
    return jax.shard_map(
        functools.partial(shards, mesh.shape["rows"], mesh.shape["cols"]),
        mesh=mesh,
        in_specs=placed,
        out_specs=P(("parts", "rows", "cols"), None),
        check_vma=False,
    )
```

time: 170 us -> 80.2 us (0.47)
  the two profiles are of different devices: /device:TPU:66 before, /device:TPU:65 now
where the time goes in v1:
time: 80.2 us; the launch traced here: 79.8 us
  Pallas kernels  75.9 us (95%)
  local copies, waits for them, and re-layouts  3.92 us (5%)
    pallas_call x1, Pallas kernels, shards(): pl.pallas_call(functools.partial(kernel, rows_n, cols_n, chunks), out_sha...  75.9 us
    unnamed x2, local copies, waits for them, and re-layouts  2.67 us

profile of v1, /device:TPU:65, one launch (start us, length us, event | category | flops | bytes accessed | tf_op | source)
XLA Modules:
  0.0 79.8 jit_solution(7070108684173874886)
XLA Ops:
  0.0 1.2 %reshape.3.q_bias = f32[1,384]{1,0:T(1,128)} reshape(f32[384]{0:T(512)} %param.11) | data formatting | bytes 3072 | tf_op jit(solution)/shard_map/reshape | solution.py:346
  1.2 1.4 %copy.8.pair_proj = bf16[128,16]{1,0:T(8,128)(2,1)} copy(bf16[128,16]{0,1:T(8,128)(2,1)} %param.12) | data formatting | bytes 8192 | tf_op args[5]
  2.6 75.9 %shard_map.73 = bf16[8,384]{1,0:T(8,128)(2,1)} custom-call(bf16[8,384]{1,0:T(8,128)(2,1)} %singles.1, bf16[128,128,128]{2,1,0:T(8,128)(2,1)} %pair.1, s32[8]{0:T(128)} %chain.1, bf16[384,1536]{1,0:T(8,128)(2,1)} %proj.1, f32[1,384]{1,0:T(1,128)} %reshape.3.q_bias, bf16[128,16]{1,0:T(8,128)(2,1)} %copy.8.pair_proj, bf16[384,384]{1,0:T(8,128)(2,1)} %out_proj.1), custom_call_target="tpu_custom_call" | custom-call | tf_op jit(solution)/shard_map/pallas_call | solution.py:312
  78.6 1.3 %copy.10 = bf16[8,384]{1,0:T(8,128)(2,1)} copy(bf16[8,384]{1,0:T(8,128)(2,1)} %shard_map.73) | data formatting | bytes 12288

commit v2 on v1

--- a/solution.py
+++ b/solution.py
@@ -73,12 +73,20 @@
     row_recv,
     key_send,
     key_recv,
+    up_in,
+    up_send,
+    up_recv,
+    down_in,
+    down_send,
+    down_recv,
+    twin_send,
+    twin_recv,
     part_send,
     part_recv,
 ):
     own, features = own_v.shape
     tile_rows, tile_cols, channels = pair_v.shape
-    heads = pair_proj_v.shape[1]
+    heads = pair_proj_v.shape[0]
     head_dim = features // heads
     lane_blocks = features // LANES
     slots = chain_s.shape[0]
@@ -93,7 +101,7 @@
                 (singles, own_v),
                 (pair_proj, pair_proj_v),
                 (proj, proj_v),
-                (q_bias, q_bias_v),
+                (q_bias, q_bias_v.at[0]),
                 (out_proj, out_proj_v),
                 (chain, chain_s),
             ]
@@ -114,42 +122,140 @@
     for piece in pieces[1:]:
         piece.start()
 
+    reach = cols_n // 4
+    core = lax.rem(row, 2)
+    chips = rows_n // 2
+    near = [d for n in range(reach, 0, -1) for d in (n, -n)]
+
+    def along(d):
+        return lax.rem(col + d + cols_n, cols_n)
+
+    def across(d):
+        return lax.rem(row + 2 * d, rows_n)
+
+    def mine(target):
+        return lax.rem(target, 2) == core
+
     barrier = pltpu.get_barrier_semaphore()
-    for d in range(1, cols_n):
-        pl.semaphore_signal(barrier, inc=1, **peer("cols", lax.rem(col + d, cols_n)))
-    for d in range(1, rows_n):
-        pl.semaphore_signal(barrier, inc=1, **peer("rows", lax.rem(row + d, rows_n)))
-
-    def far_first(count):
-        return sorted(range(1, count), key=lambda d: -min(d, count - d))
-
-    def send(src, dst, sems, axis, index, mine, target):
+    for d in near:
+        pl.semaphore_signal(barrier, inc=1, **peer("cols", along(d)))
+    for d in range(1, chips):
+        pl.semaphore_signal(barrier, inc=1, **peer("rows", across(d)))
+    twin = row + 1 - 2 * core
+    pl.semaphore_signal(barrier, inc=1, **peer("rows", twin))
+
+    def send(src, dst, sent, arrived, axis, index):
         return pltpu.make_async_remote_copy(
-            src_ref=src,
-            dst_ref=dst,
-            send_sem=sems[0].at[target],
-            recv_sem=sems[1].at[mine],
-            **peer(axis, index),
-        )
-
-    def query_copy(other):
+            src_ref=src, dst_ref=dst, send_sem=sent, recv_sem=arrived, **peer(axis, index)
+        )
+
+    def query_copy(slot, target, stage):
         return send(
-            query_in.at[col], query_in.at[col], (query_send, query_recv), "cols", other, col, other
-        )
-
-    def row_copy(other):
-        return send(row_in.at[row], row_in.at[row], (row_send, row_recv), "rows", other, row, other)
-
-    def key_copy(other):
-        return send(row_in.at[other], key_in.at[col], (key_send, key_recv), "cols", other, col, other)
+            query_in.at[slot],
+            query_in.at[slot],
+            query_send.at[stage, target],
+            query_recv.at[slot],
+            "cols",
+            target,
+        )
+
+    def row_copy(target):
+        return send(
+            row_in.at[row], row_in.at[row], row_send.at[target], row_recv.at[row], "rows", target
+        )
+
+    def key_copy(src, slot, target, stage):
+        return send(
+            src, key_in.at[slot], key_send.at[stage, target], key_recv.at[slot], "cols", target
+        )
+
+    def up_copy(n):
+        return send(
+            row_in.at[along(reach + 1 + n)],
+            up_in.at[n],
+            up_send.at[n],
+            up_recv.at[n],
+            "cols",
+            along(reach),
+        )
+
+    def down_copy(n):
+        return send(
+            row_in.at[along(-reach - 1 - n)],
+            down_in.at[n],
+            down_send.at[n],
+            down_recv.at[n],
+            "cols",
+            along(-reach),
+        )
+
+    def twin_copy():
+        return send(key_in, key_in, twin_send, twin_recv, "rows", twin)
 
     def part_copy(other):
         return send(
-            part_out.at[other], part_in.at[col], (part_send, part_recv), "cols", other, col, other
-        )
-
-    def arrival(buf, sems, axis, index):
-        return send(buf.at[index], buf.at[index], sems, axis, index, index, index)
+            part_out.at[other],
+            part_in.at[col],
+            part_send.at[other],
+            part_recv.at[col],
+            "cols",
+            other,
+        )
+
+    def query_stage(act):
+        for d in near:
+            act(query_copy(col, along(d), 0))
+
+    def query_relay(direction, act):
+        for n in range(reach if direction > 0 else reach - 1, 0, -1):
+            act(query_copy(along(-direction * reach), along(direction * n), 1))
+
+    def key_stage(act):
+        for n in range(reach - 1, -1, -1):
+
+            @pl.when(mine(along(reach + 1 + n)))
+            def _():
+                act(up_copy(n))
+
+            if n < reach - 1:
+
+                @pl.when(mine(along(-reach - 1 - n)))
+                def _():
+                    act(down_copy(n))
+
+        for d in near:
+            target = along(d)
+
+            @pl.when(mine(target))
+            def _():
+                act(key_copy(row_in.at[target], col, target, 0))
+
+    def key_relay(act, wait):
+        for n in range(reach - 1, -1, -1):
+            target = along(n + 1)
+
+            @pl.when(mine(target))
+            def _():
+                if wait:
+                    up_copy(n).wait_recv()
+                act(key_copy(up_in.at[n], along(-reach), target, 1))
+
+        for n in range(reach - 2, -1, -1):
+            target = along(-n - 1)
+
+            @pl.when(mine(target))
+            def _():
+                if wait:
+                    down_copy(n).wait_recv()
+                act(key_copy(down_in.at[n], along(reach), target, 1))
+
+    def start(copy):
+        copy.start()
+
+    def wait_send(copy):
+        copy.wait_send()
+
+    far_first = sorted(range(1, cols_n), key=lambda d: -min(d, cols_n - d))
 
     loads[0].wait()
     normed = normalize(own_v[...].astype(F32), -1).astype(BF16)
@@ -157,10 +263,10 @@
     row_in[pl.ds(row, 1)] = normed[None]
 
     loads[1].wait()
-    pair_w = jnp.transpose(pair_proj_v[...].astype(F32)).astype(BF16)
+    pair_w = pair_proj_v[...]
 
     def tile_bias(first, last):
-        @pl.loop(first, last, unroll=2)
+        @pl.loop(first, last, unroll=4)
         def _(i):
             block = jnp.transpose(pair_v[i]).astype(F32)
             block_normed = normalize(block, 0).astype(BF16)
@@ -173,31 +279,54 @@
             tile_bias(n * step, (n + 1) * step)
 
     bias_chunks(0, chunks // 4)
-    pl.semaphore_wait(barrier, cols_n + rows_n - 2)
-    for d in far_first(rows_n):
-        row_copy(lax.rem(row + d, rows_n)).start()
-    for d in far_first(cols_n):
-        query_copy(lax.rem(col + d, cols_n)).start()
+    pl.semaphore_wait(barrier, len(near) + chips)
+    for d in range(1, chips):
+        row_copy(across(d)).start()
+    query_stage(start)
+    bias_chunks(chunks // 4, 3 * chunks // 4)
+
+    query_copy(along(-reach), along(-reach), 0).wait_recv()
+    query_relay(1, start)
+    query_copy(along(reach), along(reach), 0).wait_recv()
+    query_relay(-1, start)
+    for d in range(1, chips):
+        send(
+            row_in.at[across(d)],
+            row_in.at[across(d)],
+            row_send.at[across(d)],
+            row_recv.at[across(d)],
+            "rows",
+            across(d),
+        ).wait_recv()
+    key_stage(start)
+
+    @pl.when(mine(col))
+    def _():
+        key_in[pl.ds(col, 1)] = row_in[pl.ds(col, 1)]
 
     loads[2].wait()
     loads[3].wait()
     own_gate = jax.nn.sigmoid(matmul(normed, proj_v[:, 3 * features :]))
-    bias_chunks(chunks // 4, chunks // 2)
-
-    for d in range(1, rows_n):
-        arrival(row_in, (row_send, row_recv), "rows", lax.rem(row + d, rows_n)).wait_recv()
-    for d in far_first(cols_n):
-        key_copy(lax.rem(col + d, cols_n)).start()
-    key_in[pl.ds(col, 1)] = row_in[pl.ds(col, 1)]
-    bias_chunks(chunks // 2, chunks)
-
-    for d in range(1, cols_n):
-        arrival(query_in, (query_send, query_recv), "cols", lax.rem(col + d, cols_n)).wait_recv()
+    bias_chunks(3 * chunks // 4, chunks)
+    key_relay(start, True)
+
+    for d in far_first:
+        if d not in (reach, cols_n - reach):
+            query_copy(along(d), along(d), 0).wait_recv()
     queries = (
         matmul(flat(query_in[...]), proj_v[:, :features]) + q_bias_v[...]
     ).astype(BF16).astype(F32)
-    for d in range(1, cols_n):
-        arrival(key_in, (key_send, key_recv), "cols", lax.rem(col + d, cols_n)).wait_recv()
+
+    @pl.when(mine(col))
+    def _():
+        for d in far_first:
+            key_copy(key_in.at[along(d)], along(d), along(d), 0).wait_recv()
+        twin_copy().start()
+
+    @pl.when(jnp.logical_not(mine(col)))
+    def _():
+        twin_copy().wait_recv()
+
     key_side = matmul(flat(key_in[...]), proj_v[:, features : 3 * features]).astype(BF16)
     keys = key_side[:, :features]
     values = key_side[:, features:].astype(F32)
@@ -272,8 +401,8 @@
         ).astype(BF16)
 
     part_in[pl.ds(col, 1)] = part_out[pl.ds(col, 1)]
-    for d in far_first(cols_n):
-        part_copy(lax.rem(col + d, cols_n)).start()
+    for d in far_first:
+        part_copy(along(d)).start()
     loads[4].wait()
     spread_row = iota((LANES, features), 0)
     spread_head = lax.div(iota((LANES, features), 1), head_dim)
@@ -281,8 +410,15 @@
     spread_group = lax.div(spread_row, heads)
     to_total = jnp.where(matches & (spread_group < 2), 1.0, 0.0).astype(BF16)
     to_top = jnp.where(matches & (spread_group >= 2) & (spread_group < 5), 1.0, 0.0).astype(BF16)
-    for d in range(1, cols_n):
-        arrival(part_in, (part_send, part_recv), "cols", lax.rem(col + d, cols_n)).wait_recv()
+    for d in far_first:
+        send(
+            part_in.at[along(d)],
+            part_in.at[along(d)],
+            part_send.at[along(d)],
+            part_recv.at[along(d)],
+            "cols",
+            along(d),
+        ).wait_recv()
     arrived = flat(part_in[:, :, features:])
     total = matmul(arrived, to_total).reshape(cols_n, own_rows, features)
     tops = matmul(arrived, to_top).reshape(cols_n, own_rows, features)
@@ -292,26 +428,34 @@
     attended = (own_gate * (numerator / total)).astype(BF16)
     out[...] = matmul(attended, out_proj_v[...]).astype(BF16)
 
-    for d in range(1, rows_n):
-        row_copy(lax.rem(row + d, rows_n)).wait_send()
-    for d in range(1, cols_n):
-        other = lax.rem(col + d, cols_n)
-        query_copy(other).wait_send()
-        key_copy(other).wait_send()
-        part_copy(other).wait_send()
+    for d in range(1, chips):
+        row_copy(across(d)).wait_send()
+    query_stage(wait_send)
+    query_relay(1, wait_send)
+    query_relay(-1, wait_send)
+    key_stage(wait_send)
+    key_relay(wait_send, False)
+
+    @pl.when(mine(col))
+    def _():
+        twin_copy().wait_send()
+
+    for d in far_first:
+        part_copy(along(d)).wait_send()
 
 
 def shards(rows_n, cols_n, singles, pair, chain_sizes, single_proj, query_bias, pair_proj, out_proj):
     own, features = singles.shape
     tile_rows, tile_cols, channels = pair.shape
     heads = pair_proj.shape[1]
-    chunks = 16
+    chunks = 8
+    reach = cols_n // 4
     dma = pltpu.SemaphoreType.DMA
     lane_blocks = features // LANES
     widest = -(-LANES // (features // heads)) + 1
     return pl.pallas_call(
         functools.partial(kernel, rows_n, cols_n, chunks),
-        out_shape=jax.ShapeDtypeStruct((own, features), BF16),
+        out_shape=pltpu.VMEM((own, features), BF16),
         in_specs=[pl.BlockSpec(memory_space=pl.ANY)] * 7,
         out_specs=pl.BlockSpec(memory_space=pltpu.VMEM),
         scratch_shapes=[
@@ -320,7 +464,7 @@
             pltpu.SMEM(chain_sizes.shape, jnp.int32),
             pltpu.VMEM(single_proj.shape, BF16),
             pltpu.VMEM((1, features), F32),
-            pltpu.VMEM(pair_proj.shape, BF16),
+            pltpu.VMEM((heads, channels), BF16),
             pltpu.VMEM(out_proj.shape, BF16),
             pltpu.VMEM((cols_n, own, features), BF16),
             pltpu.VMEM((rows_n, own, features), BF16),
@@ -333,17 +477,25 @@
             pltpu.VMEM((cols_n, own, features + LANES), BF16),
             dma((6,)),
             dma((chunks,)),
-            dma((cols_n,)),
+            dma((2, cols_n)),
             dma((cols_n,)),
             dma((rows_n,)),
             dma((rows_n,)),
+            dma((2, cols_n)),
             dma((cols_n,)),
-            dma((cols_n,)),
+            pltpu.VMEM((reach, own, features), BF16),
+            dma((reach,)),
+            dma((reach,)),
+            pltpu.VMEM((reach, own, features), BF16),
+            dma((reach,)),
+            dma((reach,)),
+            dma,
+            dma,
             dma((cols_n,)),
             dma((cols_n,)),
         ],
         compiler_params=pltpu.CompilerParams(collective_id=0, has_side_effects=True),
-    )(singles, pair, chain_sizes, single_proj, query_bias.reshape(1, features), pair_proj, out_proj)
+    )(singles, pair, chain_sizes, single_proj, query_bias, pair_proj.T, out_proj)
 
 
 def solution(mesh):

time: 80.2 us -> 75 us (0.935)
  local copies, waits for them, and re-layouts: 3.92 us -> 0.6 us
  Pallas kernels: 75.9 us -> 74.3 us
    unnamed x2 -> x1, local copies, waits for them, and re-layouts: 2.67 us -> 0.6 us
    pallas_call x1, Pallas kernels: 75.9 us -> 74.3 us  [shards(): pl.pallas_call(functools.partial(kernel, rows_n, cols_n, chunks), out_sha...]
    reshape x1 -> x0, local copies, waits for them, and re-layouts: 1.24 us -> none  [shards(): query_bias.reshape(1, features)]
where the time goes in v2:
time: 75 us; the launch traced here: 74.9 us
  Pallas kernels  74.3 us (99%)
    pallas_call x1, Pallas kernels, shards(): pl.pallas_call(functools.partial(kernel, rows_n, cols_n, chunks), out_sha...  74.3 us

profile of v2, /device:TPU:65, one launch (start us, length us, event | category | flops | bytes accessed | tf_op | source)
XLA Modules:
  0.0 74.9 jit_solution(14115664131628318566)
XLA Ops:
  0.0 74.3 %shard_map.73 = bf16[8,384]{1,0:T(8,128)(2,1)S(1)} custom-call(bf16[8,384]{1,0:T(8,128)(2,1)} %singles.1, bf16[128,128,128]{2,1,0:T(8,128)(2,1)} %pair.1, s32[8]{0:T(128)} %chain.1, bf16[384,1536]{1,0:T(8,128)(2,1)} %proj.1, f32[384]{0:T(512)} %q_bias.1, bf16[16,128]{1,0:T(8,128)(2,1)} %bitcast.1, bf16[384,384]{1,0:T(8,128)(2,1)} %out_proj.1), custom_call_target="tpu_custom_call" | custom-call | tf_op jit(solution)/shard_map/pallas_call | solution.py:456
  74.3 0.6 copy.9

commit v3 on v2

--- a/solution.py
+++ b/solution.py
@@ -14,8 +14,8 @@
 BF16 = jnp.bfloat16
 
 
-def peer(axis, index):
-    return dict(device_id={axis: index}, device_id_type=pl.DeviceIdType.MESH)
+def peer(**place):
+    return dict(device_id=place, device_id_type=pl.DeviceIdType.MESH)
 
 
 def normalize(rows, axis):
@@ -57,7 +57,6 @@
     pair_proj_v,
     out_proj_v,
     query_in,
-    row_in,
     key_in,
     bias_v,
     score_v,
@@ -69,18 +68,13 @@
     pair_sem,
     query_send,
     query_recv,
-    row_send,
-    row_recv,
     key_send,
     key_recv,
     up_in,
-    up_send,
     up_recv,
     down_in,
-    down_send,
     down_recv,
-    twin_send,
-    twin_recv,
+    relay_send,
     part_send,
     part_recv,
 ):
@@ -123,30 +117,37 @@
         piece.start()
 
     reach = cols_n // 4
-    core = lax.rem(row, 2)
-    chips = rows_n // 2
     near = [d for n in range(reach, 0, -1) for d in (n, -n)]
 
     def along(d):
         return lax.rem(col + d + cols_n, cols_n)
 
-    def across(d):
-        return lax.rem(row + 2 * d, rows_n)
-
-    def mine(target):
-        return lax.rem(target, 2) == core
+    offset = lax.rem(row - col + cols_n, cols_n)
+    diagonal = offset == 0
+    direct = (offset <= reach) | (offset >= cols_n - reach)
+    upward = (offset > reach) & (offset <= 2 * reach)
+    downward = (offset > 2 * reach) & (offset < cols_n - reach)
 
     barrier = pltpu.get_barrier_semaphore()
+
+    def announce(**place):
+        pl.semaphore_signal(barrier, inc=1, **peer(**place))
+
     for d in near:
-        pl.semaphore_signal(barrier, inc=1, **peer("cols", along(d)))
-    for d in range(1, chips):
-        pl.semaphore_signal(barrier, inc=1, **peer("rows", across(d)))
-    twin = row + 1 - 2 * core
-    pl.semaphore_signal(barrier, inc=1, **peer("rows", twin))
-
-    def send(src, dst, sent, arrived, axis, index):
+        announce(cols=along(d))
+        announce(rows=col, cols=along(d))
+    for n in range(reach):
+        announce(rows=along(n + 1), cols=along(-reach))
+        if n < reach - 1:
+            announce(rows=along(-n - 1), cols=along(reach))
+
+    @pl.when(jnp.logical_not(diagonal))
+    def _():
+        announce(rows=col)
+
+    def send(src, dst, sent, arrived, **place):
         return pltpu.make_async_remote_copy(
-            src_ref=src, dst_ref=dst, send_sem=sent, recv_sem=arrived, **peer(axis, index)
+            src_ref=src, dst_ref=dst, send_sem=sent, recv_sem=arrived, **peer(**place)
         )
 
     def query_copy(slot, target, stage):
@@ -155,42 +156,46 @@
             query_in.at[slot],
             query_send.at[stage, target],
             query_recv.at[slot],
-            "cols",
-            target,
-        )
-
-    def row_copy(target):
+            cols=target,
+        )
+
+    def key_copy(target):
         return send(
-            row_in.at[row], row_in.at[row], row_send.at[target], row_recv.at[row], "rows", target
-        )
-
-    def key_copy(src, slot, target, stage):
+            query_in.at[col],
+            key_in.at[col],
+            key_send.at[target],
+            key_recv.at[col],
+            rows=target,
+            cols=row,
+        )
+
+    def up_copy(target):
+        n = offset - reach - 1
         return send(
-            src, key_in.at[slot], key_send.at[stage, target], key_recv.at[slot], "cols", target
-        )
-
-    def up_copy(n):
+            query_in.at[col],
+            up_in.at[n],
+            key_send.at[target],
+            up_recv.at[n],
+            rows=target,
+            cols=along(reach),
+        )
+
+    def down_copy(target):
+        n = cols_n - offset - reach - 1
         return send(
-            row_in.at[along(reach + 1 + n)],
-            up_in.at[n],
-            up_send.at[n],
-            up_recv.at[n],
-            "cols",
-            along(reach),
-        )
-
-    def down_copy(n):
-        return send(
-            row_in.at[along(-reach - 1 - n)],
+            query_in.at[col],
             down_in.at[n],
-            down_send.at[n],
+            key_send.at[target],
             down_recv.at[n],
-            "cols",
-            along(-reach),
-        )
-
-    def twin_copy():
-        return send(key_in, key_in, twin_send, twin_recv, "rows", twin)
+            rows=target,
+            cols=along(-reach),
+        )
+
+    def relay_copy(src, slot, target):
+        return send(src, key_in.at[slot], relay_send.at[target], key_recv.at[slot], cols=target)
+
+    def landed(buf, sem, n):
+        send(buf.at[n], buf.at[n], relay_send.at[0], sem.at[n], cols=along(1)).wait_recv()
 
     def part_copy(other):
         return send(
@@ -198,8 +203,7 @@
             part_in.at[col],
             part_send.at[other],
             part_recv.at[col],
-            "cols",
-            other,
+            cols=other,
         )
 
     def query_stage(act):
@@ -211,43 +215,34 @@
             act(query_copy(along(-direction * reach), along(direction * n), 1))
 
     def key_stage(act):
-        for n in range(reach - 1, -1, -1):
-
-            @pl.when(mine(along(reach + 1 + n)))
+        @pl.when(direct)
+        def _():
+            for d in rows_far_first:
+                act(key_copy(lax.rem(row + d, rows_n)))
+
+            @pl.when(jnp.logical_not(diagonal))
             def _():
-                act(up_copy(n))
-
-            if n < reach - 1:
-
-                @pl.when(mine(along(-reach - 1 - n)))
-                def _():
-                    act(down_copy(n))
-
-        for d in near:
-            target = along(d)
-
-            @pl.when(mine(target))
-            def _():
-                act(key_copy(row_in.at[target], col, target, 0))
+                act(key_copy(row))
+
+        @pl.when(upward)
+        def _():
+            for d in rows_far_first + [0]:
+                act(up_copy(lax.rem(row + d, rows_n)))
+
+        @pl.when(downward)
+        def _():
+            for d in rows_far_first + [0]:
+                act(down_copy(lax.rem(row + d, rows_n)))
 
     def key_relay(act, wait):
         for n in range(reach - 1, -1, -1):
-            target = along(n + 1)
-
-            @pl.when(mine(target))
-            def _():
-                if wait:
-                    up_copy(n).wait_recv()
-                act(key_copy(up_in.at[n], along(-reach), target, 1))
-
+            if wait:
+                landed(up_in, up_recv, n)
+            act(relay_copy(up_in.at[n], along(-reach), along(n + 1)))
         for n in range(reach - 2, -1, -1):
-            target = along(-n - 1)
-
-            @pl.when(mine(target))
-            def _():
-                if wait:
-                    down_copy(n).wait_recv()
-                act(key_copy(down_in.at[n], along(reach), target, 1))
+            if wait:
+                landed(down_in, down_recv, n)
+            act(relay_copy(down_in.at[n], along(reach), along(-n - 1)))
 
     def start(copy):
         copy.start()
@@ -255,12 +250,17 @@
     def wait_send(copy):
         copy.wait_send()
 
+    rows_far_first = sorted(range(1, rows_n), key=lambda d: -min(d, rows_n - d))
     far_first = sorted(range(1, cols_n), key=lambda d: -min(d, cols_n - d))
 
     loads[0].wait()
     normed = normalize(own_v[...].astype(F32), -1).astype(BF16)
     query_in[pl.ds(col, 1)] = normed[None]
-    row_in[pl.ds(row, 1)] = normed[None]
+
+    @pl.when(diagonal)
+    def _():
+        key_in[pl.ds(col, 1)] = normed[None]
+
 
     loads[1].wait()
     pair_w = pair_proj_v[...]
@@ -278,54 +278,36 @@
             pieces[n].wait()
             tile_bias(n * step, (n + 1) * step)
 
-    bias_chunks(0, chunks // 4)
-    pl.semaphore_wait(barrier, len(near) + chips)
-    for d in range(1, chips):
-        row_copy(across(d)).start()
+    own_self = jnp.where(diagonal, 1, 0)
+    pl.semaphore_wait(barrier, len(near) + cols_n - own_self)
+    key_stage(start)
     query_stage(start)
-    bias_chunks(chunks // 4, 3 * chunks // 4)
-
-    query_copy(along(-reach), along(-reach), 0).wait_recv()
+    bias_chunks(0, chunks // 2)
+
+    landed(query_in, query_recv, along(-reach))
     query_relay(1, start)
-    query_copy(along(reach), along(reach), 0).wait_recv()
+    landed(query_in, query_recv, along(reach))
     query_relay(-1, start)
-    for d in range(1, chips):
-        send(
-            row_in.at[across(d)],
-            row_in.at[across(d)],
-            row_send.at[across(d)],
-            row_recv.at[across(d)],
-            "rows",
-            across(d),
-        ).wait_recv()
-    key_stage(start)
-
-    @pl.when(mine(col))
-    def _():
-        key_in[pl.ds(col, 1)] = row_in[pl.ds(col, 1)]
-
     loads[2].wait()
     loads[3].wait()
     own_gate = jax.nn.sigmoid(matmul(normed, proj_v[:, 3 * features :]))
+    bias_chunks(chunks // 2, 3 * chunks // 4)
+    key_relay(start, True)
     bias_chunks(3 * chunks // 4, chunks)
-    key_relay(start, True)
 
     for d in far_first:
         if d not in (reach, cols_n - reach):
-            query_copy(along(d), along(d), 0).wait_recv()
+            landed(query_in, query_recv, along(d))
     queries = (
         matmul(flat(query_in[...]), proj_v[:, :features]) + q_bias_v[...]
     ).astype(BF16).astype(F32)
 
-    @pl.when(mine(col))
+    for d in far_first:
+        landed(key_in, key_recv, along(d))
+
+    @pl.when(jnp.logical_not(diagonal))
     def _():
-        for d in far_first:
-            key_copy(key_in.at[along(d)], along(d), along(d), 0).wait_recv()
-        twin_copy().start()
-
-    @pl.when(jnp.logical_not(mine(col)))
-    def _():
-        twin_copy().wait_recv()
+        landed(key_in, key_recv, col)
 
     key_side = matmul(flat(key_in[...]), proj_v[:, features : 3 * features]).astype(BF16)
     keys = key_side[:, :features]
@@ -411,14 +393,7 @@
     to_total = jnp.where(matches & (spread_group < 2), 1.0, 0.0).astype(BF16)
     to_top = jnp.where(matches & (spread_group >= 2) & (spread_group < 5), 1.0, 0.0).astype(BF16)
     for d in far_first:
-        send(
-            part_in.at[along(d)],
-            part_in.at[along(d)],
-            part_send.at[along(d)],
-            part_recv.at[along(d)],
-            "cols",
-            along(d),
-        ).wait_recv()
+        landed(part_in, part_recv, along(d))
     arrived = flat(part_in[:, :, features:])
     total = matmul(arrived, to_total).reshape(cols_n, own_rows, features)
     tops = matmul(arrived, to_top).reshape(cols_n, own_rows, features)
@@ -428,17 +403,11 @@
     attended = (own_gate * (numerator / total)).astype(BF16)
     out[...] = matmul(attended, out_proj_v[...]).astype(BF16)
 
-    for d in range(1, chips):
-        row_copy(across(d)).wait_send()
     query_stage(wait_send)
     query_relay(1, wait_send)
     query_relay(-1, wait_send)
     key_stage(wait_send)
     key_relay(wait_send, False)
-
-    @pl.when(mine(col))
-    def _():
-        twin_copy().wait_send()
 
     for d in far_first:
         part_copy(along(d)).wait_send()
@@ -467,7 +436,6 @@
             pltpu.VMEM((heads, channels), BF16),
             pltpu.VMEM(out_proj.shape, BF16),
             pltpu.VMEM((cols_n, own, features), BF16),
-            pltpu.VMEM((rows_n, own, features), BF16),
             pltpu.VMEM((cols_n, own, features), BF16),
             pltpu.VMEM((tile_rows * heads, tile_cols), F32),
             pltpu.VMEM((heads, tile_rows, tile_cols), F32),
@@ -480,17 +448,12 @@
             dma((2, cols_n)),
             dma((cols_n,)),
             dma((rows_n,)),
-            dma((rows_n,)),
-            dma((2, cols_n)),
             dma((cols_n,)),
             pltpu.VMEM((reach, own, features), BF16),
             dma((reach,)),
-            dma((reach,)),
             pltpu.VMEM((reach, own, features), BF16),
             dma((reach,)),
-            dma((reach,)),
-            dma,
-            dma,
+            dma((cols_n,)),
             dma((cols_n,)),
             dma((cols_n,)),
         ],

time: 75 us -> 77.5 us (1.033); the launches traced: 74.9 us -> 76.6 us
  Pallas kernels: 74.3 us -> 76 us
    pallas_call x1, Pallas kernels: 74.3 us -> 76 us  [shards(): pl.pallas_call(functools.partial(kernel, rows_n, cols_n, chunks), out_sha...]
where the time goes in v3:
time: 77.5 us; the launch traced here: 76.6 us
  Pallas kernels  76 us (98%)
    pallas_call x1, Pallas kernels, shards(): pl.pallas_call(functools.partial(kernel, rows_n, cols_n, chunks), out_sha...  76 us

profile of v3, /device:TPU:65, one launch (start us, length us, event | category | flops | bytes accessed | tf_op | source)
XLA Modules:
  0.0 76.6 jit_solution(6296699707658605213)
XLA Ops:
  0.0 76.0 %shard_map.73 = bf16[8,384]{1,0:T(8,128)(2,1)S(1)} custom-call(bf16[8,384]{1,0:T(8,128)(2,1)} %singles.1, bf16[128,128,128]{2,1,0:T(8,128)(2,1)} %pair.1, s32[8]{0:T(128)} %chain.1, bf16[384,1536]{1,0:T(8,128)(2,1)} %proj.1, f32[384]{0:T(512)} %q_bias.1, bf16[16,128]{1,0:T(8,128)(2,1)} %bitcast.1, bf16[384,384]{1,0:T(8,128)(2,1)} %out_proj.1), custom_call_target="tpu_custom_call" | custom-call | tf_op jit(solution)/shard_map/pallas_call | solution.py:425
  76.0 0.6 copy.9

commit v4 on v3

--- a/solution.py
+++ b/solution.py
@@ -26,6 +26,16 @@
 
 def matmul(a, b):
     return jnp.dot(a, b, preferred_element_type=F32)
+
+
+def halves(distance):
+    if distance in (0, 1):
+        return distance + 1, -1
+    if distance == -1:
+        return -2, 1
+    first = -(-abs(distance) // 2)
+    sign = 1 if distance > 0 else -1
+    return sign * first, distance - sign * first
 
 
 def iota(shape, dim):
@@ -70,10 +80,8 @@
     query_recv,
     key_send,
     key_recv,
-    up_in,
-    up_recv,
-    down_in,
-    down_recv,
+    mid_in,
+    mid_recv,
     relay_send,
     part_send,
     part_recv,
@@ -123,10 +131,11 @@
         return lax.rem(col + d + cols_n, cols_n)
 
     offset = lax.rem(row - col + cols_n, cols_n)
-    diagonal = offset == 0
-    direct = (offset <= reach) | (offset >= cols_n - reach)
-    upward = (offset > reach) & (offset <= 2 * reach)
-    downward = (offset > 2 * reach) & (offset < cols_n - reach)
+    splits = [(d % cols_n, *halves(d)) for d in range(cols_n // 2, -cols_n // 2, -1)]
+    splits.sort(key=lambda split: -abs(split[2]))
+    hop = 0
+    for slot, first, second in splits:
+        hop = hop + jnp.where(offset == slot, first, 0)
 
     barrier = pltpu.get_barrier_semaphore()
 
@@ -135,15 +144,8 @@
 
     for d in near:
         announce(cols=along(d))
-        announce(rows=col, cols=along(d))
-    for n in range(reach):
-        announce(rows=along(n + 1), cols=along(-reach))
-        if n < reach - 1:
-            announce(rows=along(-n - 1), cols=along(reach))
-
-    @pl.when(jnp.logical_not(diagonal))
-    def _():
-        announce(rows=col)
+    for slot, first, second in splits:
+        announce(rows=along(second), cols=along(-first))
 
     def send(src, dst, sent, arrived, **place):
         return pltpu.make_async_remote_copy(
@@ -162,37 +164,21 @@
     def key_copy(target):
         return send(
             query_in.at[col],
-            key_in.at[col],
+            mid_in.at[offset],
             key_send.at[target],
-            key_recv.at[col],
+            mid_recv.at[offset],
             rows=target,
-            cols=row,
-        )
-
-    def up_copy(target):
-        n = offset - reach - 1
+            cols=along(hop),
+        )
+
+    def relay_copy(slot, first, second):
         return send(
-            query_in.at[col],
-            up_in.at[n],
-            key_send.at[target],
-            up_recv.at[n],
-            rows=target,
-            cols=along(reach),
-        )
-
-    def down_copy(target):
-        n = cols_n - offset - reach - 1
-        return send(
-            query_in.at[col],
-            down_in.at[n],
-            key_send.at[target],
-            down_recv.at[n],
-            rows=target,
-            cols=along(-reach),
-        )
-
-    def relay_copy(src, slot, target):
-        return send(src, key_in.at[slot], relay_send.at[target], key_recv.at[slot], cols=target)
+            mid_in.at[slot],
+            key_in.at[along(-first)],
+            relay_send.at[slot],
+            key_recv.at[along(-first)],
+            cols=along(second),
+        )
 
     def landed(buf, sem, n):
         send(buf.at[n], buf.at[n], relay_send.at[0], sem.at[n], cols=along(1)).wait_recv()
@@ -215,34 +201,14 @@
             act(query_copy(along(-direction * reach), along(direction * n), 1))
 
     def key_stage(act):
-        @pl.when(direct)
-        def _():
-            for d in rows_far_first:
-                act(key_copy(lax.rem(row + d, rows_n)))
-
-            @pl.when(jnp.logical_not(diagonal))
-            def _():
-                act(key_copy(row))
-
-        @pl.when(upward)
-        def _():
-            for d in rows_far_first + [0]:
-                act(up_copy(lax.rem(row + d, rows_n)))
-
-        @pl.when(downward)
-        def _():
-            for d in rows_far_first + [0]:
-                act(down_copy(lax.rem(row + d, rows_n)))
+        for d in rows_far_first + [0]:
+            act(key_copy(lax.rem(row + d, rows_n)))
 
     def key_relay(act, wait):
-        for n in range(reach - 1, -1, -1):
+        for slot, first, second in splits:
             if wait:
-                landed(up_in, up_recv, n)
-            act(relay_copy(up_in.at[n], along(-reach), along(n + 1)))
-        for n in range(reach - 2, -1, -1):
-            if wait:
-                landed(down_in, down_recv, n)
-            act(relay_copy(down_in.at[n], along(reach), along(-n - 1)))
+                landed(mid_in, mid_recv, slot)
+            act(relay_copy(slot, first, second))
 
     def start(copy):
         copy.start()
@@ -256,11 +222,6 @@
     loads[0].wait()
     normed = normalize(own_v[...].astype(F32), -1).astype(BF16)
     query_in[pl.ds(col, 1)] = normed[None]
-
-    @pl.when(diagonal)
-    def _():
-        key_in[pl.ds(col, 1)] = normed[None]
-
 
     loads[1].wait()
     pair_w = pair_proj_v[...]
@@ -278,8 +239,7 @@
             pieces[n].wait()
             tile_bias(n * step, (n + 1) * step)
 
-    own_self = jnp.where(diagonal, 1, 0)
-    pl.semaphore_wait(barrier, len(near) + cols_n - own_self)
+    pl.semaphore_wait(barrier, len(near) + len(splits))
     key_stage(start)
     query_stage(start)
     bias_chunks(0, chunks // 2)
@@ -302,12 +262,8 @@
         matmul(flat(query_in[...]), proj_v[:, :features]) + q_bias_v[...]
     ).astype(BF16).astype(F32)
 
-    for d in far_first:
+    for d in far_first + [0]:
         landed(key_in, key_recv, along(d))
-
-    @pl.when(jnp.logical_not(diagonal))
-    def _():
-        landed(key_in, key_recv, col)
 
     key_side = matmul(flat(key_in[...]), proj_v[:, features : 3 * features]).astype(BF16)
     keys = key_side[:, :features]
@@ -449,10 +405,8 @@
             dma((cols_n,)),
             dma((rows_n,)),
             dma((cols_n,)),
-            pltpu.VMEM((reach, own, features), BF16),
-            dma((reach,)),
-            pltpu.VMEM((reach, own, features), BF16),
-            dma((reach,)),
+            pltpu.VMEM((cols_n, own, features), BF16),
+            dma((cols_n,)),
             dma((cols_n,)),
             dma((cols_n,)),
             dma((cols_n,)),

time: 77.5 us -> 78.6 us (1.014)
  Pallas kernels: 76 us -> 77.9 us
    pallas_call x1, Pallas kernels: 76 us -> 77.9 us  [shards(): pl.pallas_call(functools.partial(kernel, rows_n, cols_n, chunks), out_sha...]
where the time goes in v4:
time: 78.6 us; the launch traced here: 78.5 us
  Pallas kernels  77.9 us (99%)
    pallas_call x1, Pallas kernels, shards(): pl.pallas_call(functools.partial(kernel, rows_n, cols_n, chunks), out_sha...  77.9 us

profile of v4, /device:TPU:65, one launch (start us, length us, event | category | flops | bytes accessed | tf_op | source)
XLA Modules:
  0.0 78.5 jit_solution(18274948031793304062)
XLA Ops:
  0.0 77.9 %shard_map.73 = bf16[8,384]{1,0:T(8,128)(2,1)S(1)} custom-call(bf16[8,384]{1,0:T(8,128)(2,1)} %singles.1, bf16[128,128,128]{2,1,0:T(8,128)(2,1)} %pair.1, s32[8]{0:T(128)} %chain.1, bf16[384,1536]{1,0:T(8,128)(2,1)} %proj.1, f32[384]{0:T(512)} %q_bias.1, bf16[16,128]{1,0:T(8,128)(2,1)} %bitcast.1, bf16[384,384]{1,0:T(8,128)(2,1)} %out_proj.1), custom_call_target="tpu_custom_call" | custom-call | tf_op jit(solution)/shard_map/pallas_call | solution.py:381
  77.9 0.6 copy.9

commit v5 on v2

--- a/solution.py
+++ b/solution.py
@@ -61,6 +61,8 @@
     key_in,
     bias_v,
     score_v,
+    stack_v,
+    ones_v,
     weight_v,
     value_v,
     part_out,
@@ -192,14 +194,36 @@
     def twin_copy():
         return send(key_in, key_in, twin_send, twin_recv, "rows", twin)
 
-    def part_copy(other):
-        return send(
-            part_out.at[other],
-            part_in.at[col],
-            part_send.at[other],
-            part_recv.at[col],
+    def part_copy(piece, other):
+        tiles = pl.ds(piece, 1 if piece < lane_blocks - 1 else 2)
+        return send(
+            part_out.at[other, tiles],
+            part_in.at[col, tiles],
+            part_send.at[piece, other],
+            part_recv.at[piece, col],
             "cols",
             other,
+        )
+
+    def part_arrival(piece, other):
+        tiles = pl.ds(piece, 1 if piece < lane_blocks - 1 else 2)
+        return send(
+            part_in.at[other, tiles],
+            part_in.at[other, tiles],
+            part_send.at[piece, other],
+            part_recv.at[piece, other],
+            "cols",
+            other,
+        )
+
+    def row_arrival(target):
+        return send(
+            row_in.at[target],
+            row_in.at[target],
+            row_send.at[target],
+            row_recv.at[target],
+            "rows",
+            target,
         )
 
     def query_stage(act):
@@ -210,25 +234,25 @@
         for n in range(reach if direction > 0 else reach - 1, 0, -1):
             act(query_copy(along(-direction * reach), along(direction * n), 1))
 
-    def key_stage(act):
+    def key_stage(act, wait):
+        def pass_on(target, copy):
+            @pl.when(mine(target))
+            def _():
+                if wait:
+
+                    @pl.when(target != row)
+                    def _():
+                        row_arrival(target).wait_recv()
+
+                act(copy)
+
         for n in range(reach - 1, -1, -1):
-
-            @pl.when(mine(along(reach + 1 + n)))
-            def _():
-                act(up_copy(n))
-
+            pass_on(along(reach + 1 + n), up_copy(n))
             if n < reach - 1:
-
-                @pl.when(mine(along(-reach - 1 - n)))
-                def _():
-                    act(down_copy(n))
-
+                pass_on(along(-reach - 1 - n), down_copy(n))
         for d in near:
             target = along(d)
-
-            @pl.when(mine(target))
-            def _():
-                act(key_copy(row_in.at[target], col, target, 0))
+            pass_on(target, key_copy(row_in.at[target], col, target, 0))
 
     def key_relay(act, wait):
         for n in range(reach - 1, -1, -1):
@@ -278,37 +302,60 @@
             pieces[n].wait()
             tile_bias(n * step, (n + 1) * step)
 
-    bias_chunks(0, chunks // 4)
     pl.semaphore_wait(barrier, len(near) + chips)
     for d in range(1, chips):
         row_copy(across(d)).start()
     query_stage(start)
-    bias_chunks(chunks // 4, 3 * chunks // 4)
+    bias_chunks(0, chunks // 2)
 
     query_copy(along(-reach), along(-reach), 0).wait_recv()
     query_relay(1, start)
     query_copy(along(reach), along(reach), 0).wait_recv()
     query_relay(-1, start)
-    for d in range(1, chips):
-        send(
-            row_in.at[across(d)],
-            row_in.at[across(d)],
-            row_send.at[across(d)],
-            row_recv.at[across(d)],
-            "rows",
-            across(d),
-        ).wait_recv()
-    key_stage(start)
+    key_stage(start, True)
 
     @pl.when(mine(col))
     def _():
+        @pl.when(col != row)
+        def _():
+            row_arrival(col).wait_recv()
+
         key_in[pl.ds(col, 1)] = row_in[pl.ds(col, 1)]
 
     loads[2].wait()
     loads[3].wait()
     own_gate = jax.nn.sigmoid(matmul(normed, proj_v[:, 3 * features :]))
+    bias_chunks(chunks // 2, 3 * chunks // 4)
+    key_relay(start, True)
     bias_chunks(3 * chunks // 4, chunks)
-    key_relay(start, True)
+
+    def blocks_of(h):
+        return range(h * head_dim // LANES, ((h + 1) * head_dim - 1) // LANES + 1)
+
+    def head_lanes(b, h):
+        feature = iota((1, LANES), 1) + b * LANES
+        return (feature >= h * head_dim) & (feature < (h + 1) * head_dim)
+
+    def lanes_of(b):
+        return slice(b * LANES, (b + 1) * LANES)
+
+    members = [[h for h in range(heads) if b in blocks_of(h)] for b in range(lane_blocks)]
+    fresh = [[h for h in members[b] if blocks_of(h)[0] == b] for b in range(lane_blocks)]
+    crossing = [[h for h in fresh[b] if blocks_of(h)[-1] > b] for b in range(lane_blocks)]
+
+    loads[5].wait()
+    live = chain_s[0]
+    for n in range(1, slots - 1):
+        live = live + chain_s[n]
+    key_live = iota((1, tile_cols), 1) + col * tile_cols < live
+    lane = iota((1, LANES), 1)
+    ones_head = lax.div(iota((heads * tile_cols, LANES), 0), tile_cols)
+    ones_lane = iota((heads * tile_cols, LANES), 1)
+    ones_v[...] = jnp.where(
+        (lax.rem(ones_lane, heads) == ones_head) & (ones_lane < 2 * heads), 1.0, 0.0
+    ).astype(BF16)
+    for h in range(heads):
+        score_v[h] = jnp.where(key_live, bias_v[pl.ds(h, tile_rows, stride=heads), :], MASKED)
 
     for d in far_first:
         if d not in (reach, cols_n - reach):
@@ -316,6 +363,15 @@
     queries = (
         matmul(flat(query_in[...]), proj_v[:, :features]) + q_bias_v[...]
     ).astype(BF16).astype(F32)
+    for b in range(lane_blocks):
+        for n, h in enumerate(fresh[b]):
+            stack_v[b, n * tile_rows : (n + 1) * tile_rows, :] = jnp.where(
+                head_lanes(b, h), queries[:, lanes_of(b)], 0.0
+            ).astype(BF16)
+        for n, h in enumerate(crossing[b], len(fresh[b])):
+            stack_v[b, n * tile_rows : (n + 1) * tile_rows, :] = jnp.where(
+                head_lanes(b + 1, h), queries[:, lanes_of(b + 1)], 0.0
+            ).astype(BF16)
 
     @pl.when(mine(col))
     def _():
@@ -331,55 +387,46 @@
     keys = key_side[:, :features]
     values = key_side[:, features:].astype(F32)
 
-    def heads_of(b):
-        return [
-            h
-            for h in range(heads)
-            if h * head_dim < (b + 1) * LANES and (h + 1) * head_dim > b * LANES
-        ]
-
-    def head_lanes(b, h):
-        feature = iota((1, LANES), 1) + b * LANES
-        return (feature >= h * head_dim) & (feature < (h + 1) * head_dim)
-
-    seen = set()
+    def against_keys(stacked, b):
+        return lax.dot_general(
+            stacked, keys[:, lanes_of(b)], (((1,), (1,)), ((), ())), preferred_element_type=F32
+        )
+
+    own_rows = tile_rows // cols_n
+    top = jnp.zeros((tile_rows, LANES), F32)
+    summed_weights = jnp.zeros((tile_rows, LANES), F32)
     for b in range(lane_blocks):
-        members = heads_of(b)
-        block = slice(b * LANES, (b + 1) * LANES)
-        stacked = jnp.concatenate(
-            [jnp.where(head_lanes(b, h), queries[:, block], 0.0).astype(BF16) for h in members], axis=0
-        )
-        scores = lax.dot_general(
-            stacked, keys[:, block], (((1,), (1,)), ((), ())), preferred_element_type=F32
-        )
-        for n, h in enumerate(members):
-            part = scores[n * tile_rows : (n + 1) * tile_rows]
-            score_v[h] = score_v[h] + part if h in seen else part
-            seen.add(h)
+        count = len(fresh[b])
+        raw = against_keys(stack_v[b, : count * tile_rows, :], b)
+        if crossing[b]:
+            extra = against_keys(
+                stack_v[b, count * tile_rows : (count + len(crossing[b])) * tile_rows, :], b + 1
+            )
+        for n, h in enumerate(fresh[b]):
+            scores = raw[n * tile_rows : (n + 1) * tile_rows]
+            if h in crossing[b]:
+                at = crossing[b].index(h) * tile_rows
+                scores = scores + extra[at : at + tile_rows]
+            scores = scores * scale + score_v[h]
+            largest = jnp.maximum(jnp.max(scores, axis=-1, keepdims=True), FLOOR)
+            weight_v[:, h * tile_cols : (h + 1) * tile_cols] = jnp.exp(scores - largest).astype(BF16)
+            top = jnp.where(lax.rem(lane, heads) == h, largest, top)
+        for n, h in enumerate(members[b]):
             value_v[b, n * tile_cols : (n + 1) * tile_cols, :] = jnp.where(
-                head_lanes(b, h), values[:, block], 0.0
+                head_lanes(b, h), values[:, lanes_of(b)], 0.0
             ).astype(BF16)
-
-    loads[5].wait()
-    live = chain_s[0]
-    for n in range(1, slots - 1):
-        live = live + chain_s[n]
-    key_live = iota((1, tile_cols), 1) + col * tile_cols < live
-    lane = iota((1, LANES), 1)
-    top = jnp.zeros((tile_rows, LANES), F32)
-    for h in range(heads):
-        scores = score_v[h] * scale + bias_v[pl.ds(h, tile_rows, stride=heads), :]
-        scores = jnp.where(key_live, scores, MASKED)
-        largest = jnp.maximum(jnp.max(scores, axis=-1, keepdims=True), FLOOR)
-        weight_v[:, h * tile_cols : (h + 1) * tile_cols] = jnp.exp(scores - largest).astype(BF16)
-        top = jnp.where(lax.rem(lane, heads) == h, largest, top)
-
-    ones_row = lax.div(iota((heads * tile_cols, LANES), 0), tile_cols)
-    ones_lane = iota((heads * tile_cols, LANES), 1)
-    ones = jnp.where(
-        (lax.rem(ones_lane, heads) == ones_row) & (ones_lane < 2 * heads), 1.0, 0.0
-    ).astype(BF16)
-    stats = jnp.where(lane < 2 * heads, matmul(weight_v[...], ones), top)
+        summed = matmul(
+            weight_v[:, members[b][0] * tile_cols : (members[b][-1] + 1) * tile_cols],
+            value_v[b, : len(members[b]) * tile_cols, :],
+        )
+        part_out[:, b] = summed.reshape(cols_n, own_rows, LANES).astype(BF16)
+        span = slice(fresh[b][0] * tile_cols, (fresh[b][-1] + 1) * tile_cols)
+        summed_weights = summed_weights + matmul(weight_v[:, span], ones_v[span, :])
+        if b < lane_blocks - 1:
+            for d in far_first:
+                part_copy(b, along(d)).start()
+
+    stats = jnp.where(lane < 2 * heads, summed_weights, top)
     first = stats.astype(BF16).astype(F32)
     second = (stats - first).astype(BF16).astype(F32)
     third = stats - first - second
@@ -387,22 +434,11 @@
     stats = jnp.where(
         (group == 0) | (group == 2), first, jnp.where((group == 1) | (group == 3), second, third)
     )
-    stats = jnp.where(group < 5, stats, 0.0).astype(BF16)
-    own_rows = tile_rows // cols_n
-    part_out[:, :, features:] = stats.astype(F32).reshape(cols_n, own_rows, LANES).astype(BF16)
-    for b in range(lane_blocks):
-        members = heads_of(b)
-        summed = matmul(
-            weight_v[:, members[0] * tile_cols : (members[-1] + 1) * tile_cols],
-            value_v[b, : len(members) * tile_cols, :],
-        )
-        part_out[:, :, b * LANES : (b + 1) * LANES] = summed.reshape(
-            cols_n, own_rows, LANES
-        ).astype(BF16)
-
+    stats = jnp.where(group < 5, stats, 0.0)
+    part_out[:, lane_blocks] = stats.reshape(cols_n, own_rows, LANES).astype(BF16)
+    for d in far_first:
+        part_copy(lane_blocks - 1, along(d)).start()
     part_in[pl.ds(col, 1)] = part_out[pl.ds(col, 1)]
-    for d in far_first:
-        part_copy(along(d)).start()
     loads[4].wait()
     spread_row = iota((LANES, features), 0)
     spread_head = lax.div(iota((LANES, features), 1), head_dim)
@@ -411,20 +447,20 @@
     to_total = jnp.where(matches & (spread_group < 2), 1.0, 0.0).astype(BF16)
     to_top = jnp.where(matches & (spread_group >= 2) & (spread_group < 5), 1.0, 0.0).astype(BF16)
     for d in far_first:
-        send(
-            part_in.at[along(d)],
-            part_in.at[along(d)],
-            part_send.at[along(d)],
-            part_recv.at[along(d)],
-            "cols",
-            along(d),
-        ).wait_recv()
-    arrived = flat(part_in[:, :, features:])
+        for piece in range(lane_blocks):
+            part_arrival(piece, along(d)).wait_recv()
+    arrived = flat(part_in[:, lane_blocks])
     total = matmul(arrived, to_total).reshape(cols_n, own_rows, features)
     tops = matmul(arrived, to_top).reshape(cols_n, own_rows, features)
     factor = jnp.exp(tops - jnp.max(tops, axis=0, keepdims=True))
     total = jnp.sum(factor * total, axis=0)
-    numerator = jnp.sum(factor * part_in[:, :, :features].astype(F32), axis=0)
+    numerator = jnp.concatenate(
+        [
+            jnp.sum(factor[:, :, lanes_of(b)] * part_in[:, b].astype(F32), axis=0)
+            for b in range(lane_blocks)
+        ],
+        axis=-1,
+    )
     attended = (own_gate * (numerator / total)).astype(BF16)
     out[...] = matmul(attended, out_proj_v[...]).astype(BF16)
 
@@ -433,7 +469,7 @@
     query_stage(wait_send)
     query_relay(1, wait_send)
     query_relay(-1, wait_send)
-    key_stage(wait_send)
+    key_stage(wait_send, False)
     key_relay(wait_send, False)
 
     @pl.when(mine(col))
@@ -441,7 +477,8 @@
         twin_copy().wait_send()
 
     for d in far_first:
-        part_copy(along(d)).wait_send()
+        for piece in range(lane_blocks):
+            part_copy(piece, along(d)).wait_send()
 
 
 def shards(rows_n, cols_n, singles, pair, chain_sizes, single_proj, query_bias, pair_proj, out_proj):
@@ -471,10 +508,12 @@
             pltpu.VMEM((cols_n, own, features), BF16),
             pltpu.VMEM((tile_rows * heads, tile_cols), F32),
             pltpu.VMEM((heads, tile_rows, tile_cols), F32),
+            pltpu.VMEM((lane_blocks, widest * tile_rows, LANES), BF16),
+            pltpu.VMEM((heads * tile_cols, LANES), BF16),
             pltpu.VMEM((tile_rows, heads * tile_cols), BF16),
             pltpu.VMEM((lane_blocks, widest * tile_cols, LANES), BF16),
-            pltpu.VMEM((cols_n, own, features + LANES), BF16),
-            pltpu.VMEM((cols_n, own, features + LANES), BF16),
+            pltpu.VMEM((cols_n, lane_blocks + 1, own, LANES), BF16),
+            pltpu.VMEM((cols_n, lane_blocks + 1, own, LANES), BF16),
             dma((6,)),
             dma((chunks,)),
             dma((2, cols_n)),
@@ -491,8 +530,8 @@
             dma((reach,)),
             dma,
             dma,
-            dma((cols_n,)),
-            dma((cols_n,)),
+            dma((lane_blocks, cols_n)),
+            dma((lane_blocks, cols_n)),
         ],
         compiler_params=pltpu.CompilerParams(collective_id=0, has_side_effects=True),
     )(singles, pair, chain_sizes, single_proj, query_bias, pair_proj.T, out_proj)

time: 75 us -> 75.9 us (1.012)
  Pallas kernels: 74.3 us -> 75.2 us
    pallas_call x1, Pallas kernels: 74.3 us -> 75.2 us  [shards(): pl.pallas_call(functools.partial(kernel, rows_n, cols_n, chunks), out_sha...]
where the time goes in v5:
time: 75.9 us; the launch traced here: 75.8 us
  Pallas kernels  75.2 us (99%)
    pallas_call x1, Pallas kernels, shards(): pl.pallas_call(functools.partial(kernel, rows_n, cols_n, chunks), out_sha...  75.2 us

profile of v5, /device:TPU:65, one launch (start us, length us, event | category | flops | bytes accessed | tf_op | source)
XLA Modules:
  0.0 75.8 jit_solution(14170670527329749818)
XLA Ops:
  0.0 75.2 %shard_map.73 = bf16[8,384]{1,0:T(8,128)(2,1)S(1)} custom-call(bf16[8,384]{1,0:T(8,128)(2,1)} %singles.1, bf16[128,128,128]{2,1,0:T(8,128)(2,1)} %pair.1, s32[8]{0:T(128)} %chain.1, bf16[384,1536]{1,0:T(8,128)(2,1)} %proj.1, f32[384]{0:T(512)} %q_bias.1, bf16[16,128]{1,0:T(8,128)(2,1)} %bitcast.1, bf16[384,384]{1,0:T(8,128)(2,1)} %out_proj.1), custom_call_target="tpu_custom_call" | custom-call | tf_op jit(solution)/shard_map/pallas_call | solution.py:493
  75.2 0.6 copy.9

commit v6 on v5

--- a/solution.py
+++ b/solution.py
@@ -82,7 +82,6 @@
     down_send,
     down_recv,
     twin_send,
-    twin_recv,
     part_send,
     part_recv,
 ):
@@ -110,19 +109,18 @@
         )
     ]
     step = tile_rows // chunks
-    pieces = [
-        pltpu.make_async_copy(
-            pair.at[pl.ds(n * step, step)], pair_v.at[pl.ds(n * step, step)], pair_sem.at[n]
-        )
-        for n in range(chunks)
-    ]
+
+    def piece(n):
+        rows = pl.ds(pl.multiple_of(n * step, step), step)
+        return pltpu.make_async_copy(pair.at[rows], pair_v.at[rows], pair_sem.at[n])
+
     loads[0].start()
     loads[1].start()
-    pieces[0].start()
+    piece(0).start()
     for load in loads[2:]:
         load.start()
-    for piece in pieces[1:]:
-        piece.start()
+    for n in range(1, chunks):
+        piece(n).start()
 
     reach = cols_n // 4
     core = lax.rem(row, 2)
@@ -191,8 +189,10 @@
             along(-reach),
         )
 
-    def twin_copy():
-        return send(key_in, key_in, twin_send, twin_recv, "rows", twin)
+    def twin_copy(slot):
+        return send(
+            key_in.at[slot], key_in.at[slot], twin_send.at[slot], key_recv.at[slot], "rows", twin
+        )
 
     def part_copy(piece, other):
         tiles = pl.ds(piece, 1 if piece < lane_blocks - 1 else 2)
@@ -289,30 +289,28 @@
     loads[1].wait()
     pair_w = pair_proj_v[...]
 
-    def tile_bias(first, last):
-        @pl.loop(first, last, unroll=4)
-        def _(i):
-            block = jnp.transpose(pair_v[i]).astype(F32)
-            block_normed = normalize(block, 0).astype(BF16)
-            bias = matmul(pair_w, block_normed)
-            bias_v[pl.ds(pl.multiple_of(i * heads, heads), heads), :] = bias.astype(BF16).astype(F32)
-
     def bias_chunks(first, last):
-        for n in range(first, last):
-            pieces[n].wait()
-            tile_bias(n * step, (n + 1) * step)
-
+        @pl.loop(first, last)
+        def _(n):
+            piece(n).wait()
+            for m in range(step):
+                i = n * step + m
+                block = jnp.transpose(pair_v[i]).astype(F32)
+                bias = matmul(pair_w, normalize(block, 0).astype(BF16))
+                bias_v[pl.ds(pl.multiple_of(i * heads, heads), heads), :] = bias.astype(BF16).astype(F32)
+
+    bias_chunks(0, chunks // 4)
     pl.semaphore_wait(barrier, len(near) + chips)
     for d in range(1, chips):
         row_copy(across(d)).start()
     query_stage(start)
-    bias_chunks(0, chunks // 2)
-
+    bias_chunks(chunks // 4, 3 * chunks // 4)
+
+    key_stage(start, True)
     query_copy(along(-reach), along(-reach), 0).wait_recv()
     query_relay(1, start)
     query_copy(along(reach), along(reach), 0).wait_recv()
     query_relay(-1, start)
-    key_stage(start, True)
 
     @pl.when(mine(col))
     def _():
@@ -325,9 +323,8 @@
     loads[2].wait()
     loads[3].wait()
     own_gate = jax.nn.sigmoid(matmul(normed, proj_v[:, 3 * features :]))
-    bias_chunks(chunks // 2, 3 * chunks // 4)
+    bias_chunks(3 * chunks // 4, chunks)
     key_relay(start, True)
-    bias_chunks(3 * chunks // 4, chunks)
 
     def blocks_of(h):
         return range(h * head_dim // LANES, ((h + 1) * head_dim - 1) // LANES + 1)
@@ -375,13 +372,15 @@
 
     @pl.when(mine(col))
     def _():
+        twin_copy(col).start()
         for d in far_first:
             key_copy(key_in.at[along(d)], along(d), along(d), 0).wait_recv()
-        twin_copy().start()
+            twin_copy(along(d)).start()
 
     @pl.when(jnp.logical_not(mine(col)))
     def _():
-        twin_copy().wait_recv()
+        for d in range(cols_n):
+            twin_copy(along(d)).wait_recv()
 
     key_side = matmul(flat(key_in[...]), proj_v[:, features : 3 * features]).astype(BF16)
     keys = key_side[:, :features]
@@ -474,7 +473,8 @@
 
     @pl.when(mine(col))
     def _():
-        twin_copy().wait_send()
+        for d in range(cols_n):
+            twin_copy(along(d)).wait_send()
 
     for d in far_first:
         for piece in range(lane_blocks):
@@ -528,8 +528,7 @@
             pltpu.VMEM((reach, own, features), BF16),
             dma((reach,)),
             dma((reach,)),
-            dma,
-            dma,
+            dma((cols_n,)),
             dma((lane_blocks, cols_n)),
             dma((lane_blocks, cols_n)),
         ],

time: 75.9 us -> 75.2 us (level)
  no operation moved by 1% of the time
where the time goes in v6:
time: 75.2 us; the launch traced here: 75.1 us
  Pallas kernels  74.5 us (99%)
    pallas_call x1, Pallas kernels, shards(): pl.pallas_call(functools.partial(kernel, rows_n, cols_n, chunks), out_sha...  74.5 us

profile of v6, /device:TPU:65, one launch (start us, length us, event | category | flops | bytes accessed | tf_op | source)
XLA Modules:
  0.0 75.1 jit_solution(18433335609367718456)
XLA Ops:
  0.0 74.5 %shard_map.73 = bf16[8,384]{1,0:T(8,128)(2,1)S(1)} custom-call(bf16[8,384]{1,0:T(8,128)(2,1)} %singles.1, bf16[128,128,128]{2,1,0:T(8,128)(2,1)} %pair.1, s32[8]{0:T(128)} %chain.1, bf16[384,1536]{1,0:T(8,128)(2,1)} %proj.1, f32[384]{0:T(512)} %q_bias.1, bf16[16,128]{1,0:T(8,128)(2,1)} %bitcast.1, bf16[384,384]{1,0:T(8,128)(2,1)} %out_proj.1), custom_call_target="tpu_custom_call" | custom-call | tf_op jit(solution)/shard_map/pallas_call | solution.py:493
  74.5 0.6 copy.9

commit v7 on v6

--- a/solution.py
+++ b/solution.py
@@ -75,12 +75,8 @@
     row_recv,
     key_send,
     key_recv,
-    up_in,
-    up_send,
-    up_recv,
-    down_in,
-    down_send,
-    down_recv,
+    ready_up,
+    ready_down,
     twin_send,
     part_send,
     part_recv,
@@ -164,29 +160,9 @@
             row_in.at[row], row_in.at[row], row_send.at[target], row_recv.at[row], "rows", target
         )
 
-    def key_copy(src, slot, target, stage):
-        return send(
-            src, key_in.at[slot], key_send.at[stage, target], key_recv.at[slot], "cols", target
-        )
-
-    def up_copy(n):
-        return send(
-            row_in.at[along(reach + 1 + n)],
-            up_in.at[n],
-            up_send.at[n],
-            up_recv.at[n],
-            "cols",
-            along(reach),
-        )
-
-    def down_copy(n):
-        return send(
-            row_in.at[along(-reach - 1 - n)],
-            down_in.at[n],
-            down_send.at[n],
-            down_recv.at[n],
-            "cols",
-            along(-reach),
+    def key_copy(src, slot, target):
+        return send(
+            row_in.at[src], key_in.at[slot], key_send.at[target], key_recv.at[slot], "cols", target
         )
 
     def twin_copy(slot):
@@ -194,24 +170,22 @@
             key_in.at[slot], key_in.at[slot], twin_send.at[slot], key_recv.at[slot], "rows", twin
         )
 
-    def part_copy(piece, other):
-        tiles = pl.ds(piece, 1 if piece < lane_blocks - 1 else 2)
-        return send(
-            part_out.at[other, tiles],
-            part_in.at[col, tiles],
-            part_send.at[piece, other],
-            part_recv.at[piece, col],
+    def part_copy(other):
+        return send(
+            part_out.at[other],
+            part_in.at[col],
+            part_send.at[other],
+            part_recv.at[col],
             "cols",
             other,
         )
 
-    def part_arrival(piece, other):
-        tiles = pl.ds(piece, 1 if piece < lane_blocks - 1 else 2)
-        return send(
-            part_in.at[other, tiles],
-            part_in.at[other, tiles],
-            part_send.at[piece, other],
-            part_recv.at[piece, other],
+    def part_arrival(other):
+        return send(
+            part_in.at[other],
+            part_in.at[other],
+            part_send.at[other],
+            part_recv.at[other],
             "cols",
             other,
         )
@@ -234,6 +208,8 @@
         for n in range(reach if direction > 0 else reach - 1, 0, -1):
             act(query_copy(along(-direction * reach), along(direction * n), 1))
 
+    far_first = sorted(range(1, cols_n), key=lambda d: -min(d, cols_n - d))
+
     def key_stage(act, wait):
         def pass_on(target, copy):
             @pl.when(mine(target))
@@ -246,32 +222,11 @@
 
                 act(copy)
 
-        for n in range(reach - 1, -1, -1):
-            pass_on(along(reach + 1 + n), up_copy(n))
-            if n < reach - 1:
-                pass_on(along(-reach - 1 - n), down_copy(n))
-        for d in near:
-            target = along(d)
-            pass_on(target, key_copy(row_in.at[target], col, target, 0))
-
-    def key_relay(act, wait):
-        for n in range(reach - 1, -1, -1):
-            target = along(n + 1)
-
-            @pl.when(mine(target))
-            def _():
-                if wait:
-                    up_copy(n).wait_recv()
-                act(key_copy(up_in.at[n], along(-reach), target, 1))
-
-        for n in range(reach - 2, -1, -1):
-            target = along(-n - 1)
-
-            @pl.when(mine(target))
-            def _():
-                if wait:
-                    down_copy(n).wait_recv()
-                act(key_copy(down_in.at[n], along(reach), target, 1))
+        if wait:
+            pl.semaphore_wait(ready_up, 1)
+            pl.semaphore_wait(ready_down, 1)
+        for d in far_first:
+            pass_on(along(d), key_copy(along(d), col, along(d)))
 
     def start(copy):
         copy.start()
@@ -279,7 +234,6 @@
     def wait_send(copy):
         copy.wait_send()
 
-    far_first = sorted(range(1, cols_n), key=lambda d: -min(d, cols_n - d))
 
     loads[0].wait()
     normed = normalize(own_v[...].astype(F32), -1).astype(BF16)
@@ -303,8 +257,10 @@
     pl.semaphore_wait(barrier, len(near) + chips)
     for d in range(1, chips):
         row_copy(across(d)).start()
+    pl.semaphore_signal(ready_up, inc=1, **peer("cols", along(-reach)))
+    pl.semaphore_signal(ready_down, inc=1, **peer("cols", along(reach)))
     query_stage(start)
-    bias_chunks(chunks // 4, 3 * chunks // 4)
+    bias_chunks(chunks // 4, 5 * chunks // 8)
 
     key_stage(start, True)
     query_copy(along(-reach), along(-reach), 0).wait_recv()
@@ -323,8 +279,7 @@
     loads[2].wait()
     loads[3].wait()
     own_gate = jax.nn.sigmoid(matmul(normed, proj_v[:, 3 * features :]))
-    bias_chunks(3 * chunks // 4, chunks)
-    key_relay(start, True)
+    bias_chunks(5 * chunks // 8, chunks)
 
     def blocks_of(h):
         return range(h * head_dim // LANES, ((h + 1) * head_dim - 1) // LANES + 1)
@@ -374,7 +329,7 @@
     def _():
         twin_copy(col).start()
         for d in far_first:
-            key_copy(key_in.at[along(d)], along(d), along(d), 0).wait_recv()
+            key_copy(along(d), along(d), along(d)).wait_recv()
             twin_copy(along(d)).start()
 
     @pl.when(jnp.logical_not(mine(col)))
@@ -421,9 +376,6 @@
         part_out[:, b] = summed.reshape(cols_n, own_rows, LANES).astype(BF16)
         span = slice(fresh[b][0] * tile_cols, (fresh[b][-1] + 1) * tile_cols)
         summed_weights = summed_weights + matmul(weight_v[:, span], ones_v[span, :])
-        if b < lane_blocks - 1:
-            for d in far_first:
-                part_copy(b, along(d)).start()
 
     stats = jnp.where(lane < 2 * heads, summed_weights, top)
     first = stats.astype(BF16).astype(F32)
@@ -436,7 +388,7 @@
     stats = jnp.where(group < 5, stats, 0.0)
     part_out[:, lane_blocks] = stats.reshape(cols_n, own_rows, LANES).astype(BF16)
     for d in far_first:
-        part_copy(lane_blocks - 1, along(d)).start()
+        part_copy(along(d)).start()
     part_in[pl.ds(col, 1)] = part_out[pl.ds(col, 1)]
     loads[4].wait()
     spread_row = iota((LANES, features), 0)
@@ -446,8 +398,7 @@
     to_total = jnp.where(matches & (spread_group < 2), 1.0, 0.0).astype(BF16)
     to_top = jnp.where(matches & (spread_group >= 2) & (spread_group < 5), 1.0, 0.0).astype(BF16)
     for d in far_first:
-        for piece in range(lane_blocks):
-            part_arrival(piece, along(d)).wait_recv()
+        part_arrival(along(d)).wait_recv()
     arrived = flat(part_in[:, lane_blocks])
     total = matmul(arrived, to_total).reshape(cols_n, own_rows, features)
     tops = matmul(arrived, to_top).reshape(cols_n, own_rows, features)
@@ -469,7 +420,6 @@
     query_relay(1, wait_send)
     query_relay(-1, wait_send)
     key_stage(wait_send, False)
-    key_relay(wait_send, False)
 
     @pl.when(mine(col))
     def _():
@@ -477,8 +427,7 @@
             twin_copy(along(d)).wait_send()
 
     for d in far_first:
-        for piece in range(lane_blocks):
-            part_copy(piece, along(d)).wait_send()
+        part_copy(along(d)).wait_send()
 
 
 def shards(rows_n, cols_n, singles, pair, chain_sizes, single_proj, query_bias, pair_proj, out_proj):
@@ -486,7 +435,6 @@
     tile_rows, tile_cols, channels = pair.shape
     heads = pair_proj.shape[1]
     chunks = 8
-    reach = cols_n // 4
     dma = pltpu.SemaphoreType.DMA
     lane_blocks = features // LANES
     widest = -(-LANES // (features // heads)) + 1
@@ -520,17 +468,13 @@
             dma((cols_n,)),
             dma((rows_n,)),
             dma((rows_n,)),
-            dma((2, cols_n)),
-            dma((cols_n,)),
-            pltpu.VMEM((reach, own, features), BF16),
-            dma((reach,)),
-            dma((reach,)),
-            pltpu.VMEM((reach, own, features), BF16),
-            dma((reach,)),
-            dma((reach,)),
-            dma((cols_n,)),
-            dma((lane_blocks, cols_n)),
-            dma((lane_blocks, cols_n)),
+            dma((cols_n,)),
+            dma((cols_n,)),
+            pltpu.SemaphoreType.REGULAR,
+            pltpu.SemaphoreType.REGULAR,
+            dma((cols_n,)),
+            dma((cols_n,)),
+            dma((cols_n,)),
         ],
         compiler_params=pltpu.CompilerParams(collective_id=0, has_side_effects=True),
     )(singles, pair, chain_sizes, single_proj, query_bias, pair_proj.T, out_proj)

time: 75.2 us -> 71.5 us (0.951)
  Pallas kernels: 74.5 us -> 70.7 us
    pallas_call x1, Pallas kernels: 74.5 us -> 70.7 us  [shards(): pl.pallas_call(functools.partial(kernel, rows_n, cols_n, chunks), out_sha...]
where the time goes in v7:
time: 71.5 us; the launch traced here: 71.3 us
  Pallas kernels  70.7 us (99%)
    pallas_call x1, Pallas kernels, shards(): pl.pallas_call(functools.partial(kernel, rows_n, cols_n, chunks), out_sha...  70.7 us

profile of v7, /device:TPU:65, one launch (start us, length us, event | category | flops | bytes accessed | tf_op | source)
XLA Modules:
  0.0 71.3 jit_solution(3115938781158980837)
XLA Ops:
  0.0 70.7 %shard_map.73 = bf16[8,384]{1,0:T(8,128)(2,1)S(1)} custom-call(bf16[8,384]{1,0:T(8,128)(2,1)} %singles.1, bf16[128,128,128]{2,1,0:T(8,128)(2,1)} %pair.1, s32[8]{0:T(128)} %chain.1, bf16[384,1536]{1,0:T(8,128)(2,1)} %proj.1, f32[384]{0:T(512)} %q_bias.1, bf16[16,128]{1,0:T(8,128)(2,1)} %bitcast.1, bf16[384,384]{1,0:T(8,128)(2,1)} %out_proj.1), custom_call_target="tpu_custom_call" | custom-call | tf_op jit(solution)/shard_map/pallas_call | solution.py:441
  70.7 0.6 copy.9

commit v8 on v7

--- a/solution.py
+++ b/solution.py
@@ -328,7 +328,7 @@
     @pl.when(mine(col))
     def _():
         twin_copy(col).start()
-        for d in far_first:
+        for d in reversed(far_first):
             key_copy(along(d), along(d), along(d)).wait_recv()
             twin_copy(along(d)).start()
 
@@ -361,14 +361,18 @@
             if h in crossing[b]:
                 at = crossing[b].index(h) * tile_rows
                 scores = scores + extra[at : at + tile_rows]
-            scores = scores * scale + score_v[h]
-            largest = jnp.maximum(jnp.max(scores, axis=-1, keepdims=True), FLOOR)
-            weight_v[:, h * tile_cols : (h + 1) * tile_cols] = jnp.exp(scores - largest).astype(BF16)
-            top = jnp.where(lax.rem(lane, heads) == h, largest, top)
+            score_v[h] = scores * scale + score_v[h]
         for n, h in enumerate(members[b]):
             value_v[b, n * tile_cols : (n + 1) * tile_cols, :] = jnp.where(
                 head_lanes(b, h), values[:, lanes_of(b)], 0.0
             ).astype(BF16)
+    for b in range(lane_blocks):
+        for h in fresh[b]:
+            scores = score_v[h]
+            largest = jnp.maximum(jnp.max(scores, axis=-1, keepdims=True), FLOOR)
+            weight_v[:, h * tile_cols : (h + 1) * tile_cols] = jnp.exp(scores - largest).astype(BF16)
+            top = jnp.where(lax.rem(lane, heads) == h, largest, top)
+    for b in range(lane_blocks):
         summed = matmul(
             weight_v[:, members[b][0] * tile_cols : (members[b][-1] + 1) * tile_cols],
             value_v[b, : len(members[b]) * tile_cols, :],

time: 71.5 us -> 71 us (level)
  no operation moved by 1% of the time
where the time goes in v8:
time: 71 us; the launch traced here: 70.9 us
  Pallas kernels  70.3 us (99%)
    pallas_call x1, Pallas kernels, shards(): pl.pallas_call(functools.partial(kernel, rows_n, cols_n, chunks), out_sha...  70.3 us

profile of v8, /device:TPU:65, one launch (start us, length us, event | category | flops | bytes accessed | tf_op | source)
XLA Modules:
  0.0 70.9 jit_solution(222658489111347104)
XLA Ops:
  0.0 70.3 %shard_map.73 = bf16[8,384]{1,0:T(8,128)(2,1)S(1)} custom-call(bf16[8,384]{1,0:T(8,128)(2,1)} %singles.1, bf16[128,128,128]{2,1,0:T(8,128)(2,1)} %pair.1, s32[8]{0:T(128)} %chain.1, bf16[384,1536]{1,0:T(8,128)(2,1)} %proj.1, f32[384]{0:T(512)} %q_bias.1, bf16[16,128]{1,0:T(8,128)(2,1)} %bitcast.1, bf16[384,384]{1,0:T(8,128)(2,1)} %out_proj.1), custom_call_target="tpu_custom_call" | custom-call | tf_op jit(solution)/shard_map/pallas_call | solution.py:445
  70.3 0.6 copy.9
